TPU v7x, 8 devices: a whole 2x2x1 slice. The times are simulated.
8 devices in a mesh: dp: 2 (over z, y), tp: 4 (over x, core).
Axes of the slice: x: 2, y: 2, z: 1, core: 2. Of those that a mesh axis runs over, the one named last changes fastest.
Arguments:
- tokens: bfloat16 [4, 264, 1024], P('dp', 'tp')
- grad_y: bfloat16 [4, 264, 1024], P('dp', 'tp')
- valid_len: int32 [4], P('dp')
- norm1_gain: float32 [2, 1024], replicated
- norm1_bias: float32 [2, 1024], replicated
- w_qkv: bfloat16 [2, 3, 1024, 16, 64], P(None, None, None, 'tp')
- b_qkv: float32 [2, 3, 16, 64], P(None, None, 'tp')
- w_proj: bfloat16 [2, 16, 64, 1024], P(None, 'tp')
- b_proj: float32 [2, 1024], replicated
- layer_scale1: float32 [2, 1024], replicated
- norm2_gain: float32 [2, 1024], replicated
- norm2_bias: float32 [2, 1024], replicated
- w_up: bfloat16 [2, 2, 1024, 4096], P(None, None, None, 'tp')
- b_up: float32 [2, 2, 4096], P(None, None, 'tp')
- w_down: bfloat16 [2, 4096, 1024], P(None, 'tp')
- b_down: float32 [2, 1024], replicated
- layer_scale2: float32 [2, 1024], replicated
Outputs:
- output 1: bfloat16 [4, 264, 1024], P('dp', 'tp')
- output 2: bfloat16 [4, 264, 1024], P('dp', 'tp')
- output 3: float32 [2, 1024], replicated
- output 4: float32 [2, 1024], replicated
- output 5: float32 [2, 3, 1024, 16, 64], P(None, None, None, 'tp')
- output 6: float32 [2, 3, 16, 64], P(None, None, 'tp')
- output 7: float32 [2, 16, 64, 1024], P(None, 'tp')
- output 8: float32 [2, 1024], replicated
- output 9: float32 [2, 1024], replicated
- output 10: float32 [2, 1024], replicated
- output 11: float32 [2, 1024], replicated
- output 12: float32 [2, 2, 1024, 4096], P(None, None, None, 'tp')
- output 13: float32 [2, 2, 4096], P(None, None, 'tp')
- output 14: float32 [2, 4096, 1024], P(None, 'tp')
- output 15: float32 [2, 1024], replicated
- output 16: float32 [2, 1024], replicated
All inputs are finite; a program needn't handle non-finite values.
Results may differ from a plain program's by a relative error of at most 0.02.
Values are sent between devices in bfloat16 or wider.
A program may use at most 1 GiB of HBM per device.

v0:
```python
import jax
import jax.numpy as jnp
from jax import lax
from jax.sharding import PartitionSpec as P

NORM_EPS = 1e-6
NEG_BIG = -1e9
SHARED_SLOTS = (0, 1, 5, 6, 7, 8, 12, 13)
SPLIT_SLOTS = (2, 3, 4, 9, 10, 11)


def norm_fwd(x_tok, norm_gain, norm_shift):
    x_f32 = x_tok.astype(jnp.float32)
    centered = x_f32 - jnp.mean(x_f32, axis=-1, keepdims=True)
    inv_std = lax.rsqrt(jnp.mean(centered * centered, axis=-1, keepdims=True) + NORM_EPS)
    x_hat = centered * inv_std
    return (x_hat * norm_gain + norm_shift).astype(jnp.bfloat16), x_hat, inv_std


def norm_bwd(grad_out, x_hat, inv_std, norm_gain):
    grad_hat = grad_out * norm_gain
    mean_one = jnp.mean(grad_hat, axis=-1, keepdims=True)
    mean_two = jnp.mean(grad_hat * x_hat, axis=-1, keepdims=True)
    grad_in = inv_std * (grad_hat - mean_one - x_hat * mean_two)
    return grad_in, jnp.sum(grad_out * x_hat, axis=(0, 1)), jnp.sum(grad_out, axis=(0, 1))


def block_fwd(x_loc, key_mask, layer_prm):
    (norm1_gain, norm1_bias, w_qkv, b_qkv, w_proj, b_proj, layer_scale1,
     norm2_gain, norm2_bias, w_up, b_up, w_down, b_down, layer_scale2) = layer_prm
    normed, hat_one, std_one = norm_fwd(x_loc, norm1_gain, norm1_bias)
    normed_full = lax.all_gather(normed, 'tp', axis=1, tiled=True)
    qkv_heads = (jnp.einsum('bnd,cdhe->cbnhe', normed_full, w_qkv, preferred_element_type=jnp.float32) + b_qkv[:, None, None]).astype(jnp.bfloat16)
    score_scale = qkv_heads.shape[-1] ** -0.5
    scores = jnp.einsum('bqhe,bkhe->bhqk', qkv_heads[0], qkv_heads[1], preferred_element_type=jnp.float32) * score_scale
    attn_probs = jax.nn.softmax(jnp.where(key_mask, scores, NEG_BIG), axis=-1)
    probs_bf = attn_probs.astype(jnp.bfloat16)
    attn_heads = jnp.einsum('bhqk,bkhe->bqhe', probs_bf, qkv_heads[2], preferred_element_type=jnp.float32).astype(jnp.bfloat16)
    proj_part = jnp.einsum('crif,ife->cre', attn_heads, w_proj, preferred_element_type=jnp.float32).astype(jnp.bfloat16)
    attn_sum = lax.psum_scatter(proj_part, 'tp', scatter_dimension=1, tiled=True).astype(jnp.float32) + b_proj
    x_mid = (x_loc.astype(jnp.float32) + layer_scale1 * attn_sum).astype(jnp.bfloat16)
    normed2, hat_two, std_two = norm_fwd(x_mid, norm2_gain, norm2_bias)
    normed2_full = lax.all_gather(normed2, 'tp', axis=1, tiled=True)
    pre_act = jnp.einsum('bnd,cdf->cbnf', normed2_full, w_up, preferred_element_type=jnp.float32) + b_up[:, None, None]
    hidden = (jax.nn.silu(pre_act[0]) * pre_act[1]).astype(jnp.bfloat16)
    mlp_part = jnp.einsum('bnf,fd->bnd', hidden, w_down, preferred_element_type=jnp.float32).astype(jnp.bfloat16)
    mlp_sum = lax.psum_scatter(mlp_part, 'tp', scatter_dimension=1, tiled=True).astype(jnp.float32) + b_down
    x_out = (x_mid.astype(jnp.float32) + layer_scale2 * mlp_sum).astype(jnp.bfloat16)
    saved_acts = (hat_one, std_one, normed_full, qkv_heads, attn_probs, probs_bf, attn_heads, attn_sum,
                  hat_two, std_two, normed2_full, pre_act, hidden, mlp_sum)
    return x_out, saved_acts


def block_bwd(grad_x, saved_acts, layer_prm):
    (norm1_gain, norm1_bias, w_qkv, b_qkv, w_proj, b_proj, layer_scale1,
     norm2_gain, norm2_bias, w_up, b_up, w_down, b_down, layer_scale2) = layer_prm
    (hat_one, std_one, normed_full, qkv_heads, attn_probs, probs_bf, attn_heads, attn_sum,
     hat_two, std_two, normed2_full, pre_act, hidden, mlp_sum) = saved_acts
    grad_res = grad_x.astype(jnp.float32)
    grad_ls2 = jnp.sum(grad_res * mlp_sum, axis=(0, 1))
    grad_mlp = layer_scale2 * grad_res
    grad_b_down = jnp.sum(grad_mlp, axis=(0, 1))
    grad_mlp_full = lax.all_gather(grad_mlp.astype(jnp.bfloat16), 'tp', axis=1, tiled=True)
    grad_w_down = jnp.einsum('bnf,bnd->fd', hidden, grad_mlp_full, preferred_element_type=jnp.float32)
    grad_hidden = jnp.einsum('bnd,fd->bnf', grad_mlp_full, w_down, preferred_element_type=jnp.float32)
    gate_pre = pre_act[0]
    lin_pre = pre_act[1]
    gate_sig = jax.nn.sigmoid(gate_pre)
    grad_gate = grad_hidden * lin_pre * gate_sig * (1.0 + gate_pre * (1.0 - gate_sig))
    grad_lin = grad_hidden * gate_pre * gate_sig
    grad_pre = jnp.stack([grad_gate, grad_lin])
    grad_b_up = jnp.sum(grad_pre, axis=(1, 2))
    grad_pre_bf = grad_pre.astype(jnp.bfloat16)
    grad_w_up = jnp.einsum('bnd,cbnf->cdf', normed2_full, grad_pre_bf, preferred_element_type=jnp.float32)
    norm2_part = jnp.einsum('cbnf,cdf->bnd', grad_pre_bf, w_up, preferred_element_type=jnp.float32).astype(jnp.bfloat16)
    grad_normed2 = lax.psum_scatter(norm2_part, 'tp', scatter_dimension=1, tiled=True).astype(jnp.float32)
    grad_from2, grad_n2g, grad_n2b = norm_bwd(grad_normed2, hat_two, std_two, norm2_gain)
    grad_mid = grad_res + grad_from2
    grad_ls1 = jnp.sum(grad_mid * attn_sum, axis=(0, 1))
    grad_attn_out = layer_scale1 * grad_mid
    grad_b_proj = jnp.sum(grad_attn_out, axis=(0, 1))
    grad_attn_full = lax.all_gather(grad_attn_out.astype(jnp.bfloat16), 'tp', axis=1, tiled=True)
    grad_w_proj = jnp.einsum('crif,cre->ife', attn_heads, grad_attn_full, preferred_element_type=jnp.float32)
    grad_attn = jnp.einsum('cre,ife->crif', grad_attn_full, w_proj, preferred_element_type=jnp.float32).astype(jnp.bfloat16)
    grad_probs = jnp.einsum('bqhe,bkhe->bhqk', grad_attn, qkv_heads[2], preferred_element_type=jnp.float32)
    grad_val = jnp.einsum('bhqk,bqhe->bkhe', probs_bf, grad_attn, preferred_element_type=jnp.float32)
    score_scale = qkv_heads.shape[-1] ** -0.5
    grad_scores = (attn_probs * (grad_probs - jnp.sum(grad_probs * attn_probs, axis=-1, keepdims=True)) * score_scale).astype(jnp.bfloat16)
    grad_query = jnp.einsum('bhqk,bkhe->bqhe', grad_scores, qkv_heads[1], preferred_element_type=jnp.float32)
    grad_key = jnp.einsum('bhqk,bqhe->bkhe', grad_scores, qkv_heads[0], preferred_element_type=jnp.float32)
    grad_qkv = jnp.stack([grad_query, grad_key, grad_val])
    grad_b_qkv = jnp.sum(grad_qkv, axis=(1, 2))
    grad_qkv_bf = grad_qkv.astype(jnp.bfloat16)
    grad_w_qkv = jnp.einsum('bnd,cbnhe->cdhe', normed_full, grad_qkv_bf, preferred_element_type=jnp.float32)
    norm1_part = jnp.einsum('cbnhe,cdhe->bnd', grad_qkv_bf, w_qkv, preferred_element_type=jnp.float32).astype(jnp.bfloat16)
    grad_normed = lax.psum_scatter(norm1_part, 'tp', scatter_dimension=1, tiled=True).astype(jnp.float32)
    grad_from1, grad_n1g, grad_n1b = norm_bwd(grad_normed, hat_one, std_one, norm1_gain)
    grad_in = (grad_mid + grad_from1).astype(jnp.bfloat16)
    layer_grads = (grad_n1g, grad_n1b, grad_w_qkv, grad_b_qkv, grad_w_proj, grad_b_proj, grad_ls1,
                   grad_n2g, grad_n2b, grad_w_up, grad_b_up, grad_w_down, grad_b_down, grad_ls2)
    return grad_in, layer_grads


def solution(mesh):
    tp_size = mesh.shape['tp']
    small_spec = P()
    act_spec = P('dp', 'tp', None)
    param_specs = (small_spec, small_spec, P(None, None, None, 'tp', None), P(None, None, 'tp', None),
                   P(None, 'tp', None, None), small_spec, small_spec, small_spec, small_spec,
                   P(None, None, None, 'tp'), P(None, None, 'tp'), P(None, 'tp', None), small_spec, small_spec)

    def device_fn(tokens, grad_y, valid_len, *params):
        num_blocks = params[0].shape[0]
        positions = jnp.arange(tokens.shape[1] * tp_size)
        key_mask = (positions[None, :] < valid_len[:, None])[:, None, None, :]
        x_cur = tokens
        saved_all = []
        for layer_idx in range(num_blocks):
            layer_prm = tuple(param_arr[layer_idx] for param_arr in params)
            x_cur, saved_acts = block_fwd(x_cur, key_mask, layer_prm)
            saved_all.append(saved_acts)
        grad_cur = grad_y
        grads_rev = []
        for layer_idx in reversed(range(num_blocks)):
            layer_prm = tuple(param_arr[layer_idx] for param_arr in params)
            grad_cur, layer_grads = block_bwd(grad_cur, saved_all[layer_idx], layer_prm)
            grads_rev.append(layer_grads)
        grads_fwd = grads_rev[::-1]
        stacked = [jnp.stack([one_grads[slot_idx] for one_grads in grads_fwd]) for slot_idx in range(len(params))]
        shared_sums = lax.psum(tuple(stacked[slot_idx] for slot_idx in SHARED_SLOTS), ('dp', 'tp'))
        split_sums = lax.psum(tuple(stacked[slot_idx] for slot_idx in SPLIT_SLOTS), 'dp')
        for out_pos, slot_idx in enumerate(SHARED_SLOTS):
            stacked[slot_idx] = shared_sums[out_pos]
        for out_pos, slot_idx in enumerate(SPLIT_SLOTS):
            stacked[slot_idx] = split_sums[out_pos]
        return (x_cur, grad_cur) + tuple(stacked)

    return jax.shard_map(device_fn, mesh=mesh, in_specs=(act_spec, act_spec, P('dp')) + param_specs,
                         out_specs=(act_spec, act_spec) + param_specs, check_vma=False)
```

profile of v0, /device:TPU:0, one launch (start us, length us, event | category | flops | bytes accessed | tf_op | source)
XLA Modules:
  0.0 1324.4 jit_solution(13535461806968348748)
XLA Ops:
  16.6 14.6 %all-gather.9.cloned.1.call-done = bf16[2,264,1024]{2,0,1:T(2,128)(2,1)} async-done(((bf16[2,66,1024]{2,0,1:T(2,128)(2,1)}), bf16[2,264,1024]{2,0,1:T(2,128)(2,1)}) %all-gather.9.cloned.1.call-update) | async-done | bytes 1081360 | tf_op jit(solution)/shard_map/all_gather | solution.py:32
  42.9 29.8 %all-reduce.22.cloned.1.call-done = bf16[2,264,1024]{2,0,1:T(2,128)(2,1)} async-done(((bf16[2,264,1024]{2,0,1:T(2,128)(2,1)}), bf16[2,264,1024]{2,0,1:T(2,128)(2,1)}) %all-reduce.22.cloned.1.call-update) | async-done | bytes 1081360
  76.3 14.2 %all-gather.11.cloned.1.call-done = bf16[2,264,1024]{2,0,1:T(2,128)(2,1)} async-done(((bf16[2,66,1024]{2,0,1:T(2,128)(2,1)}), bf16[2,264,1024]{2,0,1:T(2,128)(2,1)}) %all-gather.11.cloned.1.call-update) | async-done | bytes 1081360 | tf_op jit(solution)/shard_map/all_gather | solution.py:43
  90.5 5.1 add_bitcast_fusion.1
  99.8 31.0 %all-reduce.24.cloned.1.call-done = bf16[2,264,1024]{2,0,1:T(2,128)(2,1)} async-done(((bf16[2,264,1024]{2,0,1:T(2,128)(2,1)}), bf16[2,264,1024]{2,0,1:T(2,128)(2,1)}) %all-reduce.24.cloned.1.call-update) | async-done | bytes 1081360
  134.3 14.4 %all-gather.13.cloned.1.call-done = bf16[2,264,1024]{2,0,1:T(2,128)(2,1)} async-done(((bf16[2,66,1024]{2,0,1:T(2,128)(2,1)}), bf16[2,264,1024]{2,0,1:T(2,128)(2,1)}) %all-gather.13.cloned.1.call-update) | async-done | bytes 1081360 | tf_op jit(solution)/shard_map/all_gather | solution.py:32
  159.2 30.9 %all-reduce.26.cloned.1.call-done = bf16[2,264,1024]{2,0,1:T(2,128)(2,1)} async-done(((bf16[2,264,1024]{2,0,1:T(2,128)(2,1)}), bf16[2,264,1024]{2,0,1:T(2,128)(2,1)}) %all-reduce.26.cloned.1.call-update) | async-done | bytes 1081360
  194.4 13.4 %all-gather.15.cloned.1.call-done = bf16[2,264,1024]{2,0,1:T(2,128)(2,1)} async-done(((bf16[2,66,1024]{2,0,1:T(2,128)(2,1)}), bf16[2,264,1024]{2,0,1:T(2,128)(2,1)}) %all-gather.15.cloned.1.call-update) | async-done | bytes 1081360 | tf_op jit(solution)/shard_map/all_gather | solution.py:43
  207.8 7.0 add_bitcast_fusion
  214.8 9.0 all-gather.17.cloned.1.call-done
  228.9 6.2 bitcast_convert_fusion.3
  237.3 31.1 %all-reduce.28.cloned.1.call-done = bf16[2,264,1024]{2,0,1:T(2,128)(2,1)} async-done(((bf16[2,264,1024]{2,0,1:T(2,128)(2,1)}), bf16[2,264,1024]{2,0,1:T(2,128)(2,1)}) %all-reduce.28.cloned.1.call-update) | async-done | bytes 1081360
  274.7 14.0 %all-gather.19.cloned.1.call-done = bf16[2,264,1024]{2,0,1:T(2,128)(2,1)} async-done(((bf16[2,66,1024]{2,0,1:T(2,128)(2,1)}), bf16[2,264,1024]{2,0,1:T(2,128)(2,1)}) %all-gather.19.cloned.1.call-update) | async-done | bytes 1081360 | tf_op jit(solution)/shard_map/all_gather | solution.py:82
  297.7 6.9 fusion.133
  304.5 6.9 fusion.136
  316.7 31.1 %all-reduce.30.cloned.1.call-done = bf16[2,264,1024]{2,0,1:T(2,128)(2,1)} async-done(((bf16[2,264,1024]{2,0,1:T(2,128)(2,1)}), bf16[2,264,1024]{2,0,1:T(2,128)(2,1)}) %all-reduce.30.cloned.1.call-update) | async-done | bytes 1081360
  360.1 6.4 convolution_bitcast_fusion.2
  366.5 5.8 convolution_bitcast_fusion
  372.4 5.1 fusion.33
  377.5 6.2 bitcast_convert_fusion.2
  393.6 23.8 %all-reduce.32.cloned.1.call-done = bf16[2,264,1024]{2,0,1:T(2,128)(2,1)} async-done(((bf16[2,264,1024]{2,0,1:T(2,128)(2,1)}), bf16[2,264,1024]{2,0,1:T(2,128)(2,1)}) %all-reduce.32.cloned.1.call-update) | async-done | bytes 1081360
  423.4 6.8 convolution_bitcast_fusion.3
  433.8 6.2 pad_maximum_fusion
  448.1 6.8 fusion.127
  454.9 6.8 fusion.130
  467.5 8.5 pad_maximum_fusion.1
  492.9 9.0 all-reduce.9
  501.9 12.4 all-reduce.38.cloned.1.call-done
  524.1 725.8 %all-reduce.36.cloned.1.call-done = (f32[2,3,1024,4,64]{2,4,3,1,0:T(8,128)}, f32[2,4,64,1024]{3,2,1,0:T(8,128)}, f32[2,2,1024,1024]{2,3,1,0:T(8,128)}, f32[2,1024,1024]{2,1,0:T(8,128)}) async-done(((f32[2,3,1024,4,64]{2,4,3,1,0:T(8,128)}, f32[2,4,64,1024]{3,2,1,0:T(8,128)}, f32[2,2,1024,1024]{2,3,1,0:T(8,128)}, f32[2,1024,1024]{2,1,0:T(8,128)}), (f32[2,3,1024,4,64]{2,4,3,1,0:T(8,128)}, ...) | async-done | bytes 33554448 | tf_op jit(solution)/shard_map/psum | solution.py:131
  1249.9 16.4 %copy.100 = f32[2,2,1024,1024]{3,2,1,0:T(8,128)} copy(f32[2,2,1024,1024]{2,3,1,0:T(8,128)} %get-tuple-element.84) | data formatting | bytes 33554432
  1266.3 33.5 %all-reduce.34.cloned.1.call-done = (f32[2,1024]{1,0:T(2,128)}, f32[2,1024]{1,0:T(2,128)}, f32[2,1024]{1,0:T(2,128)}, f32[2,1024]{1,0:T(2,128)}, f32[2,1024]{1,0...) async-done(((f32[2,1024]{1,0:T(2,128)}, f32[2,1024]{1,0:T(2,128)}, f32[2,1024]{1,0:T(2,128)}, f32[2,1024]{1,0:T(2,128)}, f32[2,1024]{1,0:T(2,128)}, ...) | async-done | bytes 65552 | tf_op jit(solution)/shard_map/psum | solution.py:130
  1302.5 6.8 copy.224
  (280 shorter events, 156.9 us)
Async XLA Ops:
  7.2 24.1 %all-gather.9.cloned.1.call-start = ((), (), s32[]{:S(2)}) async-start(), calls=%async_computation | async-start | bytes 1351680 | tf_op jit(solution)/shard_map/all_gather | solution.py:32
  14.3 58.4 %all-reduce.22.cloned.1.call-start = ((), (), s32[]{:S(2)}) async-start(), calls=%async_computation.8 | async-start | bytes 2162688
  39.4 33.3 %copy-start = (bf16[2,66,1024]{2,0,1:T(2,128)(2,1)S(1)}, bf16[2,66,1024]{2,0,1:T(2,128)(2,1)}, u32[]{:S(2)}) copy-start(bf16[2,66,1024]{2,0,1:T(2,128)(2,1)} %param.17) | copy-start | bytes 811012
  41.5 34.7 %copy-start.34 = (f32[2,2,1024]{2,1,0:T(2,128)S(1)}, f32[2,2,1024]{2,1,0:T(2,128)}, u32[]{:S(2)}) copy-start(f32[2,2,1024]{2,1,0:T(2,128)} %param.30) | copy-start | bytes 49156
  41.6 48.9 %all-gather.11.cloned.1.call-start = ((), (), s32[]{:S(2)}) async-start(), calls=%async_computation.1 | async-start | bytes 1351680 | tf_op jit(solution)/shard_map/all_gather | solution.py:43
  76.0 54.8 %all-reduce.24.cloned.1.call-start = ((), (), s32[]{:S(2)}) async-start(), calls=%async_computation.9 | async-start | bytes 2162688
  99.7 48.9 %all-gather.13.cloned.1.call-start = ((), (), s32[]{:S(2)}) async-start(), calls=%async_computation.2 | async-start | bytes 1351680 | tf_op jit(solution)/shard_map/all_gather | solution.py:32
  134.2 55.8 %all-reduce.26.cloned.1.call-start = ((), (), s32[]{:S(2)}) async-start(), calls=%async_computation.10 | async-start | bytes 2162688
  158.9 34.6 %copy-start.3 = (bf16[2,66,1024]{2,0,1:T(2,128)(2,1)S(1)}, bf16[2,66,1024]{2,0,1:T(2,128)(2,1)}, u32[]{:S(2)}) copy-start(bf16[2,66,1024]{2,0,1:T(2,128)(2,1)} %param.18) | copy-start | bytes 811012
  158.9 48.9 %all-gather.15.cloned.1.call-start = ((), (), s32[]{:S(2)}) async-start(), calls=%async_computation.3 | async-start | bytes 1351680 | tf_op jit(solution)/shard_map/all_gather | solution.py:43
  193.4 30.4 %all-gather.17.cloned.1.call-start = ((), (), s32[]{:S(2)}) async-start(), calls=%async_computation.4 | async-start | bytes 1351680 | tf_op jit(solution)/shard_map/all_gather | solution.py:63
  194.4 74.0 %all-reduce.28.cloned.1.call-start = ((), (), s32[]{:S(2)}) async-start(), calls=%async_computation.11 | async-start | bytes 2162688
  237.2 51.4 %all-gather.19.cloned.1.call-start = ((), (), s32[]{:S(2)}) async-start(), calls=%async_computation.5 | async-start | bytes 1351680 | tf_op jit(solution)/shard_map/all_gather | solution.py:82
  274.2 73.6 %all-reduce.30.cloned.1.call-start = ((), (), s32[]{:S(2)}) async-start(), calls=%async_computation.12 | async-start | bytes 2162688
  316.7 55.7 %all-gather.21.cloned.1.call-start = ((), (), s32[]{:S(2)}) async-start(), calls=%async_computation.6 | async-start | bytes 1351680 | tf_op jit(solution)/shard_map/all_gather | solution.py:63
  353.5 63.8 %all-reduce.32.cloned.1.call-start = ((), (), s32[]{:S(2)}) async-start(), calls=%async_computation.13 | async-start | bytes 2162688
  385.8 54.2 %all-gather.23.cloned.1.call-start = ((), (), s32[]{:S(2)}) async-start(), calls=%async_computation.7 | async-start | bytes 1351680 | tf_op jit(solution)/shard_map/all_gather | solution.py:82
  423.1 91.2 %all-reduce.38.cloned.1.call-start = ((), (), s32[]{:S(2)}) async-start(), calls=%async_computation.16 | async-start | bytes 4325376
  423.4 6.8 copy-start.9
  423.4 6.8 copy-start.12
  423.4 6.8 copy-start.48
  423.4 10.4 slice-start.2
  467.0 9.0 copy-start.51
  467.0 9.0 copy-start.56
  467.1 782.8 %all-reduce.36.cloned.1.call-start = ((), (), s32[]{:S(2)}) async-start(), calls=%async_computation.15 | async-start | bytes 67108864 | tf_op jit(solution)/shard_map/psum | solution.py:131
  485.2 814.6 %all-reduce.34.cloned.1.call-start = ((), (), s32[]{:S(2)}) async-start(), calls=%async_computation.14 | async-start | bytes 131072 | tf_op jit(solution)/shard_map/psum | solution.py:130
  490.2 27.9 %copy-start.1 = (bf16[2,66,1024]{2,0,1:T(2,128)(2,1)S(1)}, bf16[2,66,1024]{2,0,1:T(2,128)(2,1)}, u32[]{:S(2)}) copy-start(bf16[2,66,1024]{2,0,1:T(2,128)(2,1)} %param.17) | copy-start | bytes 811012
  490.2 27.9 %copy-start.18 = (f32[2,66]{0,1:T(8,128)S(1)}, f32[2,66]{0,1:T(8,128)}, u32[]{:S(2)}) copy-start(f32[2,66]{0,1:T(8,128)} %copy-done.17) | copy-start | bytes 1588
  490.2 27.9 %copy-start.31 = (f32[2,66]{0,1:T(8,128)S(1)}, f32[2,66]{0,1:T(8,128)}, u32[]{:S(2)}) copy-start(f32[2,66]{0,1:T(8,128)} %copy-done.30) | copy-start | bytes 1588
  490.2 27.9 %copy-start.33 = (f32[1,1024]{1,0:T(1,128)S(1)}, f32[1,1024]{1,0:T(1,128)}, u32[]{:S(2)}) copy-start(f32[1,1024]{1,0:T(1,128)} %copy-done.32) | copy-start | bytes 12292
  1301.1 12.0 slice-start
  1302.5 10.5 slice-start.1
  (50 other events, 155.0 us)
Sparse Core Ops, SparseCore 0:
  14.5 16.7 all-gather.8
  41.7 30.9 all-reduce.21
  76.2 14.2 all-gather.10
  99.9 30.9 all-reduce.23
  134.3 14.2 all-gather.12
  159.0 30.9 all-reduce.25
  193.5 14.2 all-gather.14
  209.9 13.8 all-gather.16
  237.4 30.9 all-reduce.27
  274.3 14.2 all-gather.18
  316.8 30.9 all-reduce.29
  353.7 14.2 all-gather.20
  385.9 31.3 all-reduce.31
  423.3 14.2 all-gather.22
  467.2 47.0 all-reduce.37
  517.9 731.8 all-reduce.35
  1254.7 45.0 all-reduce.33
where the time goes:
time: 1330 us; the launch traced here: 1320 us
  waiting for transfers between devices  1030 us (77%)
  matrix products  133 us (10%)
  other arithmetic  72.4 us (5%)
  local copies, waits for them, and re-layouts  62.6 us (5%)
  between operations  15.7 us (1%)
    psum x1, waiting for transfers between devices, device_fn(): lax.psum(tuple((stacked[slot_idx] for slot_idx in SPLIT_SLOTS)), 'dp')  726 us
    unnamed x24, waiting for transfers between devices  190 us
    unnamed x143, local copies, waits for them, and re-layouts  42.7 us
    psum x1, waiting for transfers between devices, device_fn(): lax.psum(tuple((stacked[slot_idx] for slot_idx in SHARED_SLOTS)), ('dp',...  33.5 us
    all_gather x2, waiting for transfers between devices, block_fwd(): normed_full = lax.all_gather(normed, 'tp', axis=1, tiled=True)  29 us
    all_gather x2, waiting for transfers between devices, block_fwd(): normed2_full = lax.all_gather(normed2, 'tp', axis=1, tiled=True)  27.5 us
  transfers between devices with their start and end apart: 17, of which 15 were waited for; matrix products, arithmetic and copies ran while one was open for 8% of the time, Pallas kernels for 0%

commit v1 on v0

v1 whole, which is shorter than its diff:
```python
import jax
import jax.numpy as jnp
from jax import lax
from jax.sharding import PartitionSpec as P

NORM_EPS = 1e-6
NEG_BIG = -1e9
SHARED_SLOTS = (0, 1, 5, 6, 7, 8, 12, 13)
F32 = jnp.float32
BF16 = jnp.bfloat16


def dot(spec, a, b):
    return jnp.einsum(spec, a, b, preferred_element_type=F32)


def swap_dp(x):
    return lax.ppermute(x, 'dp', [(0, 1), (1, 0)])


def both(own, other, axis=0):
    return jnp.concatenate([own, other], axis=axis)


def norm_fwd(x_tok, norm_gain, norm_shift):
    x_f32 = x_tok.astype(F32)
    centered = x_f32 - jnp.mean(x_f32, axis=-1, keepdims=True)
    inv_std = lax.rsqrt(jnp.mean(centered * centered, axis=-1, keepdims=True) + NORM_EPS)
    x_hat = centered * inv_std
    return (x_hat * norm_gain + norm_shift).astype(BF16), x_hat, inv_std


def norm_bwd(grad_out, x_hat, inv_std, norm_gain):
    grad_hat = grad_out * norm_gain
    mean_one = jnp.mean(grad_hat, axis=-1, keepdims=True)
    mean_two = jnp.mean(grad_hat * x_hat, axis=-1, keepdims=True)
    grad_in = inv_std * (grad_hat - mean_one - x_hat * mean_two)
    return grad_in, jnp.sum(grad_out * x_hat, axis=(0, 1)), jnp.sum(grad_out, axis=(0, 1))


def gather_tp(x):
    return lax.all_gather(x, 'tp', axis=1, tiled=True)


def scatter_tp(x):
    return lax.psum_scatter(x, 'tp', scatter_dimension=1, tiled=True).astype(F32)


def attn_fwd(normed, key_mask, w_qkv, b_qkv):
    qkv = (dot('bnd,cdhe->cbnhe', normed, w_qkv) + b_qkv[:, None, None]).astype(BF16)
    scores = dot('bqhe,bkhe->bhqk', qkv[0], qkv[1]) * (qkv.shape[-1] ** -0.5)
    probs = jax.nn.softmax(jnp.where(key_mask, scores, NEG_BIG), axis=-1)
    probs_bf = probs.astype(BF16)
    heads = dot('bhqk,bkhe->bqhe', probs_bf, qkv[2]).astype(BF16)
    return heads, (qkv, probs, probs_bf)


def attn_bwd(grad_out_full, saved, w_proj):
    qkv, probs, probs_bf = saved
    grad_attn = dot('cre,ife->crif', grad_out_full, w_proj).astype(BF16)
    grad_probs = dot('bqhe,bkhe->bhqk', grad_attn, qkv[2])
    grad_val = dot('bhqk,bqhe->bkhe', probs_bf, grad_attn)
    grad_scores = (probs * (grad_probs - jnp.sum(grad_probs * probs, axis=-1, keepdims=True))
                   * (qkv.shape[-1] ** -0.5)).astype(BF16)
    grad_query = dot('bhqk,bkhe->bqhe', grad_scores, qkv[1])
    grad_key = dot('bhqk,bqhe->bkhe', grad_scores, qkv[0])
    grad_qkv = jnp.stack([grad_query, grad_key, grad_val])
    return grad_qkv.astype(BF16), jnp.sum(grad_qkv, axis=(1, 2))


def mlp_up(normed, w_up, b_up):
    pre = dot('bnd,cdf->cbnf', normed, w_up) + b_up[:, None, None]
    return pre, (jax.nn.silu(pre[0]) * pre[1]).astype(BF16)


def mlp_bwd(grad_mlp_full, pre, w_down):
    grad_hidden = dot('bnd,fd->bnf', grad_mlp_full, w_down)
    gate_sig = jax.nn.sigmoid(pre[0])
    grad_gate = grad_hidden * pre[1] * gate_sig * (1.0 + pre[0] * (1.0 - gate_sig))
    grad_lin = grad_hidden * pre[0] * gate_sig
    grad_pre = jnp.stack([grad_gate, grad_lin])
    return grad_pre.astype(BF16), jnp.sum(grad_pre, axis=(1, 2))


def block_fwd(x_loc, masks, prm):
    (norm1_gain, norm1_bias, w_qkv, b_qkv, w_proj, b_proj, layer_scale1,
     norm2_gain, norm2_bias, w_up, b_up, w_down, b_down, layer_scale2) = prm
    n1, hat_one, std_one = norm_fwd(x_loc, norm1_gain, norm1_bias)
    n1_own = gather_tp(n1)
    n1_oth = swap_dp(n1_own)
    heads_own, att_own = attn_fwd(n1_own, masks[0], w_qkv, b_qkv)
    proj_part = dot('crif,ife->cre', heads_own, w_proj).astype(BF16)
    attn_sum = scatter_tp(proj_part) + b_proj
    heads_oth, att_oth = attn_fwd(n1_oth, masks[1], w_qkv, b_qkv)
    x_mid = (x_loc.astype(F32) + layer_scale1 * attn_sum).astype(BF16)
    n2, hat_two, std_two = norm_fwd(x_mid, norm2_gain, norm2_bias)
    n2_own = gather_tp(n2)
    n2_oth = swap_dp(n2_own)
    pre_own, hid_own = mlp_up(n2_own, w_up, b_up)
    mlp_part = dot('bnf,fd->bnd', hid_own, w_down).astype(BF16)
    mlp_sum = scatter_tp(mlp_part) + b_down
    pre_oth, hid_oth = mlp_up(n2_oth, w_up, b_up)
    x_out = (x_mid.astype(F32) + layer_scale2 * mlp_sum).astype(BF16)
    saved = (hat_one, std_one, both(n1_own, n1_oth), att_own, att_oth, both(heads_own, heads_oth), attn_sum,
             hat_two, std_two, both(n2_own, n2_oth), pre_own, pre_oth, both(hid_own, hid_oth), mlp_sum)
    return x_out, saved


def block_bwd(grad_x, saved, prm):
    (norm1_gain, norm1_bias, w_qkv, b_qkv, w_proj, b_proj, layer_scale1,
     norm2_gain, norm2_bias, w_up, b_up, w_down, b_down, layer_scale2) = prm
    (hat_one, std_one, n1_all, att_own, att_oth, heads_all, attn_sum,
     hat_two, std_two, n2_all, pre_own, pre_oth, hid_all, mlp_sum) = saved
    grad_res = grad_x.astype(F32)
    grad_ls2 = jnp.sum(grad_res * mlp_sum, axis=(0, 1))
    grad_mlp = layer_scale2 * grad_res
    grad_b_down = jnp.sum(grad_mlp, axis=(0, 1))
    gm_own = gather_tp(grad_mlp.astype(BF16))
    gm_oth = swap_dp(gm_own)
    gp_own, gb_own = mlp_bwd(gm_own, pre_own, w_down)
    norm2_part = dot('cbnf,cdf->bnd', gp_own, w_up).astype(BF16)
    grad_normed2 = scatter_tp(norm2_part)
    gp_oth, gb_oth = mlp_bwd(gm_oth, pre_oth, w_down)
    grad_b_up = gb_own + gb_oth
    grad_w_down = dot('bnf,bnd->fd', hid_all, both(gm_own, gm_oth))
    grad_w_up = dot('bnd,cbnf->cdf', n2_all, both(gp_own, gp_oth, 1))
    grad_from2, grad_n2g, grad_n2b = norm_bwd(grad_normed2, hat_two, std_two, norm2_gain)
    grad_mid = grad_res + grad_from2
    grad_ls1 = jnp.sum(grad_mid * attn_sum, axis=(0, 1))
    grad_attn_out = layer_scale1 * grad_mid
    grad_b_proj = jnp.sum(grad_attn_out, axis=(0, 1))
    ga_own = gather_tp(grad_attn_out.astype(BF16))
    ga_oth = swap_dp(ga_own)
    gq_own, gbq_own = attn_bwd(ga_own, att_own, w_proj)
    norm1_part = dot('cbnhe,cdhe->bnd', gq_own, w_qkv).astype(BF16)
    grad_normed = scatter_tp(norm1_part)
    gq_oth, gbq_oth = attn_bwd(ga_oth, att_oth, w_proj)
    grad_b_qkv = gbq_own + gbq_oth
    grad_w_proj = dot('crif,cre->ife', heads_all, both(ga_own, ga_oth))
    grad_w_qkv = dot('bnd,cbnhe->cdhe', n1_all, both(gq_own, gq_oth, 1))
    grad_from1, grad_n1g, grad_n1b = norm_bwd(grad_normed, hat_one, std_one, norm1_gain)
    grad_in = (grad_mid + grad_from1).astype(BF16)
    layer_grads = (grad_n1g, grad_n1b, grad_w_qkv, grad_b_qkv, grad_w_proj, grad_b_proj, grad_ls1,
                   grad_n2g, grad_n2b, grad_w_up, grad_b_up, grad_w_down, grad_b_down, grad_ls2)
    return grad_in, layer_grads


def solution(mesh):
    tp_size = mesh.shape['tp']
    small_spec = P()
    act_spec = P('dp', 'tp', None)
    param_specs = (small_spec, small_spec, P(None, None, None, 'tp', None), P(None, None, 'tp', None),
                   P(None, 'tp', None, None), small_spec, small_spec, small_spec, small_spec,
                   P(None, None, None, 'tp'), P(None, None, 'tp'), P(None, 'tp', None), small_spec, small_spec)

    def device_fn(tokens, grad_y, valid_len, *params):
        num_blocks = params[0].shape[0]
        positions = jnp.arange(tokens.shape[1] * tp_size)
        masks = [(positions[None, :] < vl[:, None])[:, None, None, :] for vl in (valid_len, swap_dp(valid_len))]
        x_cur = tokens
        saved_all = []
        for layer_idx in range(num_blocks):
            prm = tuple(param_arr[layer_idx] for param_arr in params)
            x_cur, saved = block_fwd(x_cur, masks, prm)
            saved_all.append(saved)
        grad_cur = grad_y
        grads_rev = []
        for layer_idx in reversed(range(num_blocks)):
            prm = tuple(param_arr[layer_idx] for param_arr in params)
            grad_cur, layer_grads = block_bwd(grad_cur, saved_all[layer_idx], prm)
            grads_rev.append(layer_grads)
        grads_fwd = grads_rev[::-1]
        stacked = [jnp.stack([one_grads[slot] for one_grads in grads_fwd]) for slot in range(len(params))]
        shared_sums = lax.psum(tuple(stacked[slot] for slot in SHARED_SLOTS), ('dp', 'tp'))
        for out_pos, slot in enumerate(SHARED_SLOTS):
            stacked[slot] = shared_sums[out_pos]
        return (x_cur, grad_cur) + tuple(stacked)

    return jax.shard_map(device_fn, mesh=mesh, in_specs=(act_spec, act_spec, P('dp')) + param_specs,
                         out_specs=(act_spec, act_spec) + param_specs, check_vma=False)
```

time: 1330 us -> 656 us (0.49)
  waiting for transfers between devices: 1030 us -> 256 us
  matrix products: 133 us -> 197 us
  local copies, waits for them, and re-layouts: 62.6 us -> 80.4 us
  starting transfers between devices: 2.29 us -> 16 us
    psum x2 -> x1, waiting for transfers between devices: 759 us -> 43.3 us  [device_fn(): lax.psum(tuple((stacked[slot] for slot in SHARED_SLOTS)), ('dp', 'tp'))]
    dot_general x36 -> x56, matrix products: 133 us -> 197 us  [dot(): return jnp.einsum(spec, a, b, preferred_element_type=F32)]
    all_gather x8, waiting for transfers between devices: 79.5 us -> 33.6 us  [gather_tp(): return lax.all_gather(x, 'tp', axis=1, tiled=True)]
    unnamed x24 -> x23, waiting for transfers between devices: 190 us -> 148 us
    ppermute x0 -> x9, waiting for transfers between devices: none -> 31.5 us  [swap_dp(): return lax.ppermute(x, 'dp', [(0, 1), (1, 0)])]
    unnamed x143 -> x286, local copies, waits for them, and re-layouts: 42.7 us -> 48.9 us
  transfers between devices with their start and end apart: 17 -> 25, of which waited for: 15 -> 16; matrix products, arithmetic and copies ran while one was open for 8% -> 36% of each run, Pallas kernels for 0% -> 0%
where the time goes in v1:
time: 656 us; the launch traced here: 647 us
  waiting for transfers between devices  256 us (39%)
  matrix products  197 us (30%)
  local copies, waits for them, and re-layouts  80.4 us (12%)
  other arithmetic  80.3 us (12%)
  between operations  16.8 us (3%)
  starting transfers between devices  16 us (2%)
    dot_general x56, matrix products, dot(): return jnp.einsum(spec, a, b, preferred_element_type=F32)  197 us
    unnamed x23, waiting for transfers between devices  148 us
    unnamed x286, local copies, waits for them, and re-layouts  48.9 us
    psum x1, waiting for transfers between devices, device_fn(): lax.psum(tuple((stacked[slot] for slot in SHARED_SLOTS)), ('dp', 'tp'))  43.3 us
    all_gather x8, waiting for transfers between devices, gather_tp(): return lax.all_gather(x, 'tp', axis=1, tiled=True)  33.6 us
    ppermute x9, waiting for transfers between devices, swap_dp(): return lax.ppermute(x, 'dp', [(0, 1), (1, 0)])  31.5 us
    another operation x14, other arithmetic, device_fn(): jnp.stack([one_grads[slot] for one_grads in grads_fwd])  21.4 us
    ppermute x9, starting transfers between devices, swap_dp(): return lax.ppermute(x, 'dp', [(0, 1), (1, 0)])  13.3 us
  transfers between devices with their start and end apart: 25, of which 16 were waited for; matrix products, arithmetic and copies ran while one was open for 36% of the time, Pallas kernels for 0%

profile of v1, /device:TPU:0, one launch (start us, length us, event | category | flops | bytes accessed | tf_op | source)
XLA Modules:
  0.0 647.1 jit_solution(2748566510735437394)
XLA Ops:
  16.6 14.6 %all-gather.9.cloned.1.call-done = bf16[2,264,1024]{2,0,1:T(2,128)(2,1)} async-done(((bf16[2,66,1024]{2,0,1:T(2,128)(2,1)}), bf16[2,264,1024]{2,0,1:T(2,128)(2,1)}) %all-gather.9.cloned.1.call-update) | async-done | bytes 1081360 | tf_op jit(solution)/shard_map/all_gather | solution.py:42
  42.6 29.7 %all-reduce.19.cloned.1.call-done = bf16[2,264,1024]{2,0,1:T(2,128)(2,1)} async-done(((bf16[2,264,1024]{2,0,1:T(2,128)(2,1)}), bf16[2,264,1024]{2,0,1:T(2,128)(2,1)}) %all-reduce.19.cloned.1.call-update) | async-done | bytes 1081360
  77.3 12.8 %all-gather.11.cloned.1.call-done = bf16[2,264,1024]{2,0,1:T(2,128)(2,1)} async-done(((bf16[2,66,1024]{2,0,1:T(2,128)(2,1)}), bf16[2,264,1024]{2,0,1:T(2,128)(2,1)}) %all-gather.11.cloned.1.call-update) | async-done | bytes 1081360 | tf_op jit(solution)/shard_map/all_gather | solution.py:42
  90.1 5.1 add_bitcast_fusion.3
  110.0 29.8 %all-reduce.21.cloned.1.call-done = bf16[2,264,1024]{2,0,1:T(2,128)(2,1)} async-done(((bf16[2,264,1024]{2,0,1:T(2,128)(2,1)}), bf16[2,264,1024]{2,0,1:T(2,128)(2,1)}) %all-reduce.21.cloned.1.call-update) | async-done | bytes 1081360
  152.5 5.1 all-gather.13.cloned.1.call-done
  167.5 8.8 %collective-permute-done.6 = bf16[2,264,1024]{2,1,0:T(8,128)(2,1)} collective-permute-done((bf16[2,264,1024]{2,1,0:T(8,128)(2,1)S(1)}, bf16[2,264,1024]{2,1,0:T(8,128)(2,1)}, u32[]{:S(2)}, u32[]{:S(2)}) %collective-permute-start.6) | collective-permute-done | bytes 1081376 | tf_op jit(solution)/shard_map/ppermute | solution.py:18
  176.3 6.9 %add_bitcast_fusion.1 = f32[2,2,264,1024]{3,2,1,0:T(8,128)} fusion(f32[2,1024]{1,0:T(2,128)S(1)} %get-tuple-element.105, bf16[2,2,1024,1024]{3,2,1,0:T(8,128)(2,1)} %param.29, bf16[2,264,1024]{2,1,0:T(8,128)(2,1)} %collective-permute-done.6), kind=kOutput, calls=%fused_computation.24 | convolution fusion | flops 2215673856 | bytes 9609216 | tf_op jit(solution)/shard_map/bnd,cdf->cbnf/dot_general | solution.py:14
  185.1 13.5 %all-reduce.23.cloned.1.call-done = bf16[2,264,1024]{2,0,1:T(2,128)(2,1)} async-done(((bf16[2,264,1024]{2,0,1:T(2,128)(2,1)}), bf16[2,264,1024]{2,0,1:T(2,128)(2,1)}) %all-reduce.23.cloned.1.call-update) | async-done | bytes 1081360
  202.3 5.9 collective-permute-done.3
  241.2 24.1 %all-reduce.25.cloned.1.call-done = bf16[2,264,1024]{2,0,1:T(2,128)(2,1)} async-done(((bf16[2,264,1024]{2,0,1:T(2,128)(2,1)}), bf16[2,264,1024]{2,0,1:T(2,128)(2,1)}) %all-reduce.25.cloned.1.call-update) | async-done | bytes 1081360
  285.9 9.8 %fusion.40 = f32[1,2,1024,1024]{2,3,1,0:T(8,128)} fusion(bf16[2,2,264,1024]{3,2,1,0:T(8,128)(2,1)S(1)} %fusion.29, bf16[2,2,264,1024]{3,2,1,0:T(8,128)(2,1)S(1)} %copy-done.21, bf16[2,264,1024]{2,1,0:T(8,128)(2,1)} %collective-permute-done.8, bf16[2,264,1024]{2,1,0:T(8,128)(2,1)} %copy.77), kind=kOutput, calls=%fused_computation.67 | convolution fusion | flops 4432429056 | bytes 14876672 | tf_op jit(solution)/shard_map/bnd,cbnf->cdf/dot_general | solution.py:14
  303.7 6.1 fusion.289
  309.8 6.0 fusion.292
  321.3 7.2 %fusion.131 = f32[1,1024,1024]{2,1,0:T(8,128)} fusion(bf16[2,264,1024]{2,1,0:T(8,128)(2,1)} %collective-permute-done.7, bf16[2,264,1024]{2,1,0:T(8,128)(2,1)} %copy.80, bf16[2,264,1024]{2,1,0:T(8,128)(2,1)} %get-tuple-element.102, bf16[2,264,1024]{2,1,0:T(8,128)(2,1)} %get-tuple-element.101), kind=kOutput, calls=%fused_computation.189 | convolution fusion | flops 2216755200 | bytes 8519680 | tf_op jit(solution)/shard_map/bnf,bnd->fd/dot_general | solution.py:14
  332.1 20.7 %all-reduce.27.cloned.1.call-done = bf16[2,264,1024]{2,0,1:T(2,128)(2,1)} async-done(((bf16[2,264,1024]{2,0,1:T(2,128)(2,1)}), bf16[2,264,1024]{2,0,1:T(2,128)(2,1)}) %all-reduce.27.cloned.1.call-update) | async-done | bytes 1081360
  369.6 5.1 fusion.271
  382.5 6.2 fusion.109
  390.1 5.4 bitcast_convert_fusion.2
  399.9 5.4 fusion.185
  408.4 20.7 %all-reduce.29.cloned.1.call-done = bf16[2,264,1024]{2,0,1:T(2,128)(2,1)} async-done(((bf16[2,264,1024]{2,0,1:T(2,128)(2,1)}), bf16[2,264,1024]{2,0,1:T(2,128)(2,1)}) %all-reduce.29.cloned.1.call-update) | async-done | bytes 1081360
  437.4 6.3 multiply_bitcast_fusion.3
  446.7 7.2 %fusion.43 = f32[1,2,1024,1024]{2,3,1,0:T(8,128)S(1)} fusion(bf16[2,2,264,1024]{3,2,1,0:T(8,128)(2,1)S(1)} %fusion.31, bf16[2,2,264,1024]{3,2,1,0:T(8,128)(2,1)S(1)} %copy-done.19, bf16[2,264,1024]{2,1,0:T(8,128)(2,1)} %collective-permute-done.6, bf16[2,264,1024]{2,1,0:T(8,128)(2,1)S(1)} %copy-done.35), kind=kOutput, calls=%fused_computation.68 | convolution fusion | flops 4432429056 | bytes 14876672 | tf_op jit(solution)/shard_map/bnd,cbnf->cdf/dot_general | solution.py:14
  453.9 6.3 pad_maximum_fusion
  460.2 16.4 %copy.126 = f32[2,2,1024,1024]{3,2,1,0:T(8,128)} copy(f32[2,2,1024,1024]{2,3,1,0:T(8,128)} %pad_maximum_fusion) | data formatting | bytes 33554432
  493.5 5.8 fusion.283
  499.3 5.8 fusion.286
  517.8 15.2 %collective-permute-done.2 = bf16[2,264,1024]{2,1,0:T(8,128)(2,1)} collective-permute-done((bf16[2,264,1024]{2,1,0:T(8,128)(2,1)}, bf16[2,264,1024]{2,1,0:T(8,128)(2,1)}, u32[]{:S(2)}, u32[]{:S(2)}) %collective-permute-start.2) | collective-permute-done | bytes 1081376 | tf_op jit(solution)/shard_map/ppermute | solution.py:18
  538.4 6.0 fusion.280
  544.4 6.0 fusion.277
  554.6 9.1 %all-reduce.33.cloned.1.call-done = (bf16[2,264,1024]{2,0,1:T(2,128)(2,1)}, bf16[2,264,1024]{2,0,1:T(2,128)(2,1)}) async-done(((bf16[2,264,1024]{2,0,1:T(2,128)(2,1)}, bf16[2,264,1024]{2,0,1:T(2,128)(2,1)}), (bf16[2,264,1024]{2,0,1:T(2,128)(2,1)}, bf16[2,264,1024]{2,0,1:T(2,128)(2,1)})) %all-reduce.33.cloned.1.call-update) | async-done | bytes 2162704
  586.4 43.3 %all-reduce.31.cloned.1.call-done = (f32[2,1024]{1,0:T(2,128)}, f32[2,1024]{1,0:T(2,128)}, f32[2,1024]{1,0:T(2,128)}, f32[2,1024]{1,0:T(2,128)}, f32[2,1024]{1,0...) async-done(((f32[2,1024]{1,0:T(2,128)}, f32[2,1024]{1,0:T(2,128)}, f32[2,1024]{1,0:T(2,128)}, f32[2,1024]{1,0:T(2,128)}, f32[2,1024]{1,0:T(2,128)}, ...) | async-done | bytes 65552 | tf_op jit(solution)/shard_map/psum | solution.py:174
  (483 shorter events, 253.8 us)
Async XLA Ops:
  7.2 24.0 %all-gather.9.cloned.1.call-start = ((), (), s32[]{:S(2)}) async-start(), calls=%async_computation | async-start | bytes 1351680 | tf_op jit(solution)/shard_map/all_gather | solution.py:42
  14.3 58.0 %all-reduce.19.cloned.1.call-start = ((), (), s32[]{:S(2)}) async-start(), calls=%async_computation.8 | async-start | bytes 2162688
  15.9 182.7 %copy-start.78 = (f32[1,1024]{1,0:T(1,128)}, f32[1,1024]{1,0:T(1,128)S(1)}, u32[]{:S(2)}) copy-start(f32[1,1024]{1,0:T(1,128)S(1)} %get-tuple-element.123) | copy-start | bytes 12292
  41.2 48.9 %all-gather.11.cloned.1.call-start = ((), (), s32[]{:S(2)}) async-start(), calls=%async_computation.1 | async-start | bytes 1351680 | tf_op jit(solution)/shard_map/all_gather | solution.py:42
  41.2 157.4 %copy-start.71 = (f32[1,1024]{1,0:T(1,128)}, f32[1,1024]{1,0:T(1,128)S(1)}, u32[]{:S(2)}) copy-start(f32[1,1024]{1,0:T(1,128)S(1)} %get-tuple-element.116) | copy-start | bytes 12292
  42.6 158.2 %copy-start.72 = (f32[1,1024]{1,0:T(1,128)}, f32[1,1024]{1,0:T(1,128)S(1)}, u32[]{:S(2)}) copy-start(f32[1,1024]{1,0:T(1,128)S(1)} %get-tuple-element.108) | copy-start | bytes 12292
  73.9 65.9 %copy-start.2 = (bf16[2,66,1024]{2,0,1:T(2,128)(2,1)}, bf16[2,66,1024]{2,0,1:T(2,128)(2,1)S(1)}, u32[]{:S(2)}) copy-start(bf16[2,66,1024]{2,0,1:T(2,128)(2,1)S(1)} %get-tuple-element.90) | copy-start | bytes 811012
  75.7 30.3 %all-gather.17.cloned.1.call-start = ((), (), s32[]{:S(2)}) async-start(), calls=%async_computation.4 | async-start | bytes 1351680 | tf_op jit(solution)/shard_map/all_gather | solution.py:42
  75.8 64.0 %copy-start.69 = (f32[1,1024]{1,0:T(1,128)}, f32[1,1024]{1,0:T(1,128)S(1)}, u32[]{:S(2)}) copy-start(f32[1,1024]{1,0:T(1,128)S(1)} %get-tuple-element.113) | copy-start | bytes 12292
  76.7 63.1 %all-reduce.21.cloned.1.call-start = ((), (), s32[]{:S(2)}) async-start(), calls=%async_computation.9 | async-start | bytes 2162688
  77.3 143.2 %copy-start.98 = (f32[2,1024]{1,0:T(2,128)}, f32[2,1024]{1,0:T(2,128)S(1)}, u32[]{:S(2)}) copy-start(f32[2,1024]{1,0:T(2,128)S(1)} %get-tuple-element.104) | copy-start | bytes 24580
  99.4 58.2 %all-gather.13.cloned.1.call-start = ((), (), s32[]{:S(2)}) async-start(), calls=%async_computation.2 | async-start | bytes 1351680 | tf_op jit(solution)/shard_map/all_gather | solution.py:42
  99.4 3.6 collective-permute-start.1
  103.4 40.0 %collective-permute-start = (bf16[2,264,1024]{2,1,0:T(8,128)(2,1)S(1)}, bf16[2,264,1024]{2,1,0:T(8,128)(2,1)}, u32[]{:S(2)}, u32[]{:S(2)}) collective-permute-start(bf16[2,264,1024]{2,1,0:T(8,128)(2,1)S(1)} %copy.98), channel_id=1, source_target_pairs={{0,4},{4,0},{1,5},{5,1},{2,6},{6,2},{3,7},{7,3}} | collective-permute-start | bytes 3244040 | tf_op jit(solution)/shard_map/ppermute | solution.py:18
  108.5 169.7 %collective-permute-start.7 = (bf16[2,264,1024]{2,1,0:T(8,128)(2,1)}, bf16[2,264,1024]{2,1,0:T(8,128)(2,1)}, u32[]{:S(2)}, u32[]{:S(2)}) collective-permute-start(bf16[2,264,1024]{2,1,0:T(8,128)(2,1)} %copy.80), channel_id=1, source_target_pairs={{0,4},{4,0},{1,5},{5,1},{2,6},{6,2},{3,7},{7,3}} | collective-permute-start | bytes 3244040 | tf_op jit(solution)/shard_map/ppermute | solution.py:18
  143.2 55.4 %all-reduce.23.cloned.1.call-start = ((), (), s32[]{:S(2)}) async-start(), calls=%async_computation.10 | async-start | bytes 2162688
  151.0 25.3 %collective-permute-start.6 = (bf16[2,264,1024]{2,1,0:T(8,128)(2,1)S(1)}, bf16[2,264,1024]{2,1,0:T(8,128)(2,1)}, u32[]{:S(2)}, u32[]{:S(2)}) collective-permute-start(bf16[2,264,1024]{2,1,0:T(8,128)(2,1)S(1)} %copy.117), channel_id=1, source_target_pairs={{0,4},{4,0},{1,5},{5,1},{2,6},{6,2},{3,7},{7,3}} | collective-permute-start | bytes 3244040 | tf_op jit(solution)/shard_map/ppermute | solution.py:18
  167.4 48.9 %all-gather.15.cloned.1.call-start = ((), (), s32[]{:S(2)}) async-start(), calls=%async_computation.3 | async-start | bytes 1351680 | tf_op jit(solution)/shard_map/all_gather | solution.py:42
  183.6 24.6 %collective-permute-start.3 = (bf16[2,264,1024]{2,1,0:T(8,128)(2,1)S(1)}, bf16[2,264,1024]{2,1,0:T(8,128)(2,1)}, u32[]{:S(2)}, u32[]{:S(2)}) collective-permute-start(bf16[2,264,1024]{2,1,0:T(8,128)(2,1)S(1)} %copy.105), channel_id=1, source_target_pairs={{0,4},{4,0},{1,5},{5,1},{2,6},{6,2},{3,7},{7,3}} | collective-permute-start | bytes 3244040 | tf_op jit(solution)/shard_map/ppermute | solution.py:18
  200.2 68.0 %copy-start.4 = (bf16[2,66,1024]{2,0,1:T(2,128)(2,1)}, bf16[2,66,1024]{2,0,1:T(2,128)(2,1)S(1)}, u32[]{:S(2)}) copy-start(bf16[2,66,1024]{2,0,1:T(2,128)(2,1)S(1)} %get-tuple-element.86) | copy-start | bytes 811012
  202.0 63.4 %all-reduce.25.cloned.1.call-start = ((), (), s32[]{:S(2)}) async-start(), calls=%async_computation.11 | async-start | bytes 2162688
  219.0 54.2 %collective-permute-start.8 = (bf16[2,264,1024]{2,1,0:T(8,128)(2,1)}, bf16[2,264,1024]{2,1,0:T(8,128)(2,1)}, u32[]{:S(2)}, u32[]{:S(2)}) collective-permute-start(bf16[2,264,1024]{2,1,0:T(8,128)(2,1)} %copy.77), channel_id=1, source_target_pairs={{0,4},{4,0},{1,5},{5,1},{2,6},{6,2},{3,7},{7,3}} | collective-permute-start | bytes 3244040 | tf_op jit(solution)/shard_map/ppermute | solution.py:18
  234.4 61.3 %all-gather.19.cloned.1.call-start = ((), (), s32[]{:S(2)}) async-start(), calls=%async_computation.5 | async-start | bytes 1351680 | tf_op jit(solution)/shard_map/all_gather | solution.py:42
  273.1 79.7 %all-reduce.27.cloned.1.call-start = ((), (), s32[]{:S(2)}) async-start(), calls=%async_computation.12 | async-start | bytes 2162688
  321.2 61.2 %all-gather.21.cloned.1.call-start = ((), (), s32[]{:S(2)}) async-start(), calls=%async_computation.6 | async-start | bytes 1351680 | tf_op jit(solution)/shard_map/all_gather | solution.py:42
  329.8 30.3 %collective-permute-start.4 = (bf16[2,264,1024]{2,1,0:T(8,128)(2,1)}, bf16[2,264,1024]{2,1,0:T(8,128)(2,1)}, u32[]{:S(2)}, u32[]{:S(2)}) collective-permute-start(bf16[2,264,1024]{2,1,0:T(8,128)(2,1)} %copy.106), channel_id=1, source_target_pairs={{0,4},{4,0},{1,5},{5,1},{2,6},{6,2},{3,7},{7,3}} | collective-permute-start | bytes 3244040 | tf_op jit(solution)/shard_map/ppermute | solution.py:18
  359.7 69.4 %all-reduce.29.cloned.1.call-start = ((), (), s32[]{:S(2)}) async-start(), calls=%async_computation.13 | async-start | bytes 2162688
  397.6 90.6 %all-gather.23.cloned.1.call-start = ((), (), s32[]{:S(2)}) async-start(), calls=%async_computation.7 | async-start | bytes 1351680 | tf_op jit(solution)/shard_map/all_gather | solution.py:42
  406.6 30.9 %collective-permute-start.5 = (bf16[2,264,1024]{2,1,0:T(8,128)(2,1)}, bf16[2,264,1024]{2,1,0:T(8,128)(2,1)}, u32[]{:S(2)}, u32[]{:S(2)}) collective-permute-start(bf16[2,264,1024]{2,1,0:T(8,128)(2,1)} %copy.89), channel_id=1, source_target_pairs={{0,4},{4,0},{1,5},{5,1},{2,6},{6,2},{3,7},{7,3}} | collective-permute-start | bytes 3244040 | tf_op jit(solution)/shard_map/ppermute | solution.py:18
  434.9 128.7 %all-reduce.33.cloned.1.call-start = ((), (), s32[]{:S(2)}) async-start(), calls=%async_computation.15 | async-start | bytes 4325376
  507.7 25.3 %collective-permute-start.2 = (bf16[2,264,1024]{2,1,0:T(8,128)(2,1)}, bf16[2,264,1024]{2,1,0:T(8,128)(2,1)}, u32[]{:S(2)}, u32[]{:S(2)}) collective-permute-start(bf16[2,264,1024]{2,1,0:T(8,128)(2,1)} %copy.99), channel_id=1, source_target_pairs={{0,4},{4,0},{1,5},{5,1},{2,6},{6,2},{3,7},{7,3}} | collective-permute-start | bytes 3244040 | tf_op jit(solution)/shard_map/ppermute | solution.py:18
  517.3 112.4 %all-reduce.31.cloned.1.call-start = ((), (), s32[]{:S(2)}) async-start(), calls=%async_computation.14 | async-start | bytes 131072 | tf_op jit(solution)/shard_map/psum | solution.py:174
  (131 other events, 1346.0 us)
Sparse Core Ops, SparseCore 0:
  14.4 16.7 all-gather.8
  41.3 30.9 all-reduce.18
  75.8 14.2 all-gather.10
  92.0 13.8 all-gather.16
  108.8 30.9 all-reduce.20
  143.3 14.2 all-gather.12
  167.6 30.9 all-reduce.22
  202.1 14.2 all-gather.14
  234.5 30.8 all-reduce.24
  273.2 14.2 all-gather.18
  321.4 31.3 all-reduce.26
  359.8 14.2 all-gather.20
  397.7 31.3 all-reduce.28
  435.1 14.2 all-gather.22
  517.4 46.1 all-reduce.32
  585.9 43.7 all-reduce.30

commit v2 on v0

v2 whole, which is shorter than its diff:
```python
import jax
import jax.numpy as jnp
from jax import lax
from jax.experimental import pallas as pl
from jax.experimental.pallas import tpu as pltpu
from jax.sharding import PartitionSpec as P

NORM_EPS = 1e-6
NEG_BIG = -1e9
F32 = jnp.float32
BF16 = jnp.bfloat16
TOK = 66
PAD = 72
MESH_ID = pl.DeviceIdType.MESH


def stage_call(cid, rs, ag, local_fn, part, ins, out_shapes):
    n_seq, pad, width = ins[0].shape
    n_tp = 4
    n_in = len(ins)
    n_out = len(out_shapes)

    def kernel(*refs):
        pos = 0
        if rs:
            part_ref = refs[0]
            pos = 1
        in_refs = refs[pos:pos + n_in]
        pos += n_in
        out_refs = refs[pos:pos + n_out]
        pos += n_out
        if ag:
            full = refs[pos]
            pos += 1
        far_buf, mate_buf, peer_buf, send_buf, ssem, rsem = refs[pos:]
        dp = lax.axis_index('dp')
        t = lax.axis_index('tp')
        core = lax.rem(t, 2)
        mate = t + 1 - 2 * core
        peer = lax.rem(t + 2, n_tp)
        far = lax.rem(mate + 2, n_tp)

        def remote(src, dst, k, dev):
            return pltpu.make_async_remote_copy(src_ref=src, dst_ref=dst, send_sem=ssem.at[k], recv_sem=rsem.at[k],
                                                device_id=(dp, dev), device_id_type=MESH_ID)

        barrier = pltpu.get_barrier_semaphore()
        for dev in (mate, peer):
            pl.semaphore_signal(barrier, inc=1, device_id=(dp, dev), device_id_type=MESH_ID)
        pl.semaphore_wait(barrier, 2)

        started = []
        if rs:
            c_far = [remote(part_ref.at[b, far], far_buf.at[b], b, mate) for b in range(n_seq)]
            c_mate = [remote(part_ref.at[b, mate], mate_buf.at[b], n_seq + b, mate) for b in range(n_seq)]
            for cp in c_far + c_mate:
                cp.start()
            c_peer = []
            for b in range(n_seq):
                c_far[b].wait_recv()
                send_buf[b] = (part_ref[b, peer].astype(F32) + far_buf[b].astype(F32)).astype(BF16)
                cp = remote(send_buf.at[b], peer_buf.at[b], 2 * n_seq + b, peer)
                cp.start()
                c_peer.append(cp)
            started += c_far + c_mate + c_peer
        g_peer, g_mate = [], []
        for b in range(n_seq):
            acc = None
            if rs:
                c_mate[b].wait_recv()
                acc = part_ref[b, t].astype(F32) + mate_buf[b].astype(F32)
                c_peer[b].wait_recv()
                acc = acc + peer_buf[b].astype(F32)
            val = local_fn(b, acc, in_refs, out_refs)
            if ag:
                full[b, t] = val
                cp = remote(full.at[b, t], full.at[b, t], 3 * n_seq + b, peer)
                cp.start()
                g_peer.append(cp)
                cp = remote(full.at[b, t], full.at[b, t], 4 * n_seq + b, mate)
                cp.start()
                g_mate.append(cp)
        if ag:
            g_fwd = []
            for b in range(n_seq):
                g_peer[b].wait_recv()
                cp = remote(full.at[b, peer], full.at[b, peer], 5 * n_seq + b, mate)
                cp.start()
                g_fwd.append(cp)
            for b in range(n_seq):
                g_mate[b].wait_recv()
            for b in range(n_seq):
                g_fwd[b].wait_recv()
            started += g_peer + g_mate + g_fwd
        for cp in started:
            cp.wait_send()

    outs = list(out_shapes)
    if ag:
        outs.append(jax.ShapeDtypeStruct((n_seq, n_tp, pad, width), BF16))
    args = ([part] if rs else []) + list(ins)
    vm = pl.BlockSpec(memory_space=pltpu.VMEM)
    shard = (n_seq, pad, width)
    return pl.pallas_call(
        kernel,
        out_shape=outs,
        in_specs=[vm] * len(args),
        out_specs=[vm] * len(outs),
        scratch_shapes=[pltpu.VMEM(shard, BF16)] * 4 + [pltpu.SemaphoreType.DMA((6 * n_seq,))] * 2,
        compiler_params=pltpu.CompilerParams(collective_id=cid, has_side_effects=True, vmem_limit_bytes=24 * 2 ** 20),
        cost_estimate=pl.CostEstimate(flops=40_000_000, bytes_accessed=4_000_000, transcendentals=0),
        name=f'stage{cid}',
    )(*args)


def ln_stats(x):
    x_f32 = x.astype(F32)
    centered = x_f32 - jnp.mean(x_f32, axis=-1, keepdims=True)
    inv_std = lax.rsqrt(jnp.mean(centered * centered, axis=-1, keepdims=True) + NORM_EPS)
    return centered * inv_std, inv_std


def ln_bwd(grad_out, x, gain):
    x_hat, inv_std = ln_stats(x)
    grad_hat = grad_out * gain
    mean_one = jnp.mean(grad_hat, axis=-1, keepdims=True)
    mean_two = jnp.mean(grad_hat * x_hat, axis=-1, keepdims=True)
    return inv_std * (grad_hat - mean_one - x_hat * mean_two), x_hat


def add_rows(rows_ref, b, rows):
    for k, val in enumerate(rows):
        s = jnp.sum(val, axis=0, keepdims=True)
        rows_ref[k:k + 1, :] = s if b == 0 else rows_ref[k:k + 1, :] + s


def key_valid(rows, n_keys, seq_len):
    col = lax.broadcasted_iota(jnp.int32, (rows, n_keys), 1)
    shard = jnp.zeros_like(col)
    for k in range(1, n_keys // PAD):
        shard = shard + (col >= k * PAD).astype(jnp.int32)
    return jnp.logical_and(col - PAD * shard < TOK, col - (PAD - TOK) * shard < seq_len)


def mm(a, b, dims=((1,), (0,))):
    return lax.dot_general(a, b, (dims, ((), ())), preferred_element_type=F32)


def head_probs(q_half, k_pair, valid):
    scores = mm(q_half, k_pair, ((1,), (1,))) * 0.125
    scores = jnp.where(valid, scores, NEG_BIG)
    e = jnp.exp(scores - jnp.max(scores, axis=-1, keepdims=True))
    return e / jnp.sum(e, axis=-1, keepdims=True)


def attn_fwd_kernel(vl_ref, qkv_ref, o_ref):
    rows = qkv_ref.shape[1]
    valid = key_valid(rows, rows, vl_ref[pl.program_id(0)])
    half = lax.broadcasted_iota(jnp.int32, (rows, 128), 1) // 64
    for pair in range(2):
        cols = slice(128 * pair, 128 * pair + 128)
        q, k, v = qkv_ref[0, :, cols], qkv_ref[1, :, cols], qkv_ref[2, :, cols]
        outs = []
        for h in range(2):
            probs = head_probs(jnp.where(half == h, q, jnp.zeros_like(q)), k, valid)
            outs.append(mm(probs.astype(BF16), v))
        o_ref[:, cols] = jnp.where(half == 0, outs[0], outs[1]).astype(BF16)


def attn_bwd_kernel(vl_ref, qkv_ref, do_ref, dqkv_ref, db_ref):
    rows = qkv_ref.shape[1]
    valid = key_valid(rows, rows, vl_ref[pl.program_id(0)])
    half = lax.broadcasted_iota(jnp.int32, (rows, 128), 1) // 64

    @pl.when(pl.program_id(0) == 0)
    def _():
        db_ref[...] = jnp.zeros_like(db_ref)

    for pair in range(2):
        cols = slice(128 * pair, 128 * pair + 128)
        q, k, v = qkv_ref[0, :, cols], qkv_ref[1, :, cols], qkv_ref[2, :, cols]
        do = do_ref[:, cols]
        dq, dk, dv = [], [], []
        for h in range(2):
            probs = head_probs(jnp.where(half == h, q, jnp.zeros_like(q)), k, valid)
            grad_p = mm(jnp.where(half == h, do, jnp.zeros_like(do)), v, ((1,), (1,)))
            grad_s = (probs * (grad_p - jnp.sum(grad_p * probs, axis=-1, keepdims=True)) * 0.125).astype(BF16)
            dv.append(mm(probs.astype(BF16), do, ((0,), (0,))))
            dq.append(mm(grad_s, k))
            dk.append(mm(grad_s, q, ((0,), (0,))))
        for c, pieces in enumerate((dq, dk, dv)):
            val = jnp.where(half == 0, pieces[0], pieces[1])
            dqkv_ref[c, :, cols] = val.astype(BF16)
            db_ref[c:c + 1, cols] += jnp.sum(val, axis=0, keepdims=True)


def attn_fwd(qkv, seq_len):
    n_seq = seq_len.shape[0]
    rows = qkv.shape[1] // n_seq
    return pl.pallas_call(
        attn_fwd_kernel,
        grid=(n_seq,),
        in_specs=[pl.BlockSpec(memory_space=pltpu.SMEM), pl.BlockSpec((3, rows, 256), lambda b: (0, b, 0))],
        out_specs=pl.BlockSpec((rows, 256), lambda b: (b, 0)),
        out_shape=jax.ShapeDtypeStruct((n_seq * rows, 256), BF16),
        compiler_params=pltpu.CompilerParams(vmem_limit_bytes=24 * 2 ** 20),
        cost_estimate=pl.CostEstimate(flops=2_000_000_000, bytes_accessed=2_000_000, transcendentals=0),
        name='attn_fwd')(seq_len, qkv)


def attn_bwd(qkv, grad_o, seq_len):
    n_seq = seq_len.shape[0]
    rows = qkv.shape[1] // n_seq
    return pl.pallas_call(
        attn_bwd_kernel,
        grid=(n_seq,),
        in_specs=[pl.BlockSpec(memory_space=pltpu.SMEM), pl.BlockSpec((3, rows, 256), lambda b: (0, b, 0)),
                  pl.BlockSpec((rows, 256), lambda b: (b, 0))],
        out_specs=[pl.BlockSpec((3, rows, 256), lambda b: (0, b, 0)), pl.BlockSpec((3, 256), lambda b: (0, 0))],
        out_shape=[jax.ShapeDtypeStruct((3, n_seq * rows, 256), BF16), jax.ShapeDtypeStruct((3, 256), F32)],
        compiler_params=pltpu.CompilerParams(vmem_limit_bytes=24 * 2 ** 20, dimension_semantics=('arbitrary',)),
        cost_estimate=pl.CostEstimate(flops=4_000_000_000, bytes_accessed=3_000_000, transcendentals=0),
        name='attn_bwd')(seq_len, qkv, grad_o)


def wgrad_kernel(a0_ref, a1_ref, b0_ref, b1_ref, *rest):
    out_ref = rest[-1]
    out_ref[...] = mm(a0_ref[...], b0_ref[...], ((0,), (0,))) + mm(a1_ref[...], b1_ref[...], ((0,), (0,)))


def wgrad(layer, a_pair, b_pair, a_index, b_index, groups, n_blk, buf, name):
    rows, width = b_pair[0].shape[-2:]
    blk = 256
    a_block = (rows, blk) if a_pair[0].ndim == 2 else (pl.squeezed, rows, blk)
    b_block = (rows, width) if b_pair[0].ndim == 2 else (pl.squeezed, rows, width)
    a_spec = pl.BlockSpec(a_block, a_index)
    b_spec = pl.BlockSpec(b_block, b_index)
    out_spec = pl.BlockSpec((pl.squeezed, pl.squeezed, blk, width), lambda g, i: (layer, g, i, 0))
    args = [a_pair[0], a_pair[1], b_pair[0], b_pair[1]]
    in_specs = [a_spec, a_spec, b_spec, b_spec]
    alias = {}
    if buf is not None:
        args.append(buf)
        in_specs.append(pl.BlockSpec(memory_space=pl.ANY))
        alias = {4: 0}
    return pl.pallas_call(
        wgrad_kernel,
        grid=(groups, n_blk),
        in_specs=in_specs,
        out_specs=out_spec,
        out_shape=jax.ShapeDtypeStruct((2, groups, n_blk * blk, width), F32),
        input_output_aliases=alias,
        compiler_params=pltpu.CompilerParams(vmem_limit_bytes=32 * 2 ** 20),
        cost_estimate=pl.CostEstimate(flops=4 * rows * width * blk * groups * n_blk, bytes_accessed=8_000_000,
                                      transcendentals=0),
        name=name)(*args)


def dot(spec, a, b):
    return jnp.einsum(spec, a, b, preferred_element_type=F32)


def swap_dp(x):
    return lax.ppermute(x, 'dp', [(0, 1), (1, 0)])


def flat(x):
    return x.reshape(-1, x.shape[-1])


def shards(x):
    return x.reshape(2, 4, PAD, x.shape[-1])


def row(ref, layer):
    return ref[layer:layer + 1, :]


def gather_norm(cid, layer, x, gain, bias):
    def local(b, acc, ins, outs):
        x_ref, g_ref, b_ref = ins
        x_hat, _ = ln_stats(x_ref[b])
        return (x_hat * row(g_ref, layer) + row(b_ref, layer)).astype(BF16)
    return stage_call(cid, False, True, local, None, (x, gain, bias), [])[0]


def gather_scaled(cid, layer, g, scale):
    def local(b, acc, ins, outs):
        g_ref, s_ref = ins
        return (row(s_ref, layer) * g_ref[b].astype(F32)).astype(BF16)
    return stage_call(cid, False, True, local, None, (g, scale), [])[0]


def residual_norm(cid, layer, part, x, bias, scale, norm_layer, gain, shift):
    def local(b, acc, ins, outs):
        x_ref, b_ref, s_ref, g_ref, h_ref = ins
        total = acc + row(b_ref, layer)
        outs[1][b] = total
        x_new = (x_ref[b].astype(F32) + row(s_ref, layer) * total).astype(BF16)
        outs[0][b] = x_new
        x_hat, _ = ln_stats(x_new)
        return (x_hat * row(g_ref, norm_layer) + row(h_ref, norm_layer)).astype(BF16)
    shp = [jax.ShapeDtypeStruct(x.shape, BF16), jax.ShapeDtypeStruct(x.shape, F32)]
    return stage_call(cid, True, True, local, part, (x, bias, scale, gain, shift), shp)


def residual_last(cid, layer, part, x, bias, scale, grad_y):
    def local(b, acc, ins, outs):
        x_ref, b_ref, s_ref, g_ref = ins
        total = acc + row(b_ref, layer)
        outs[0][b] = (x_ref[b].astype(F32) + row(s_ref, layer) * total).astype(BF16)
        grad = g_ref[b].astype(F32)
        add_rows(outs[1], b, [grad * total, row(s_ref, layer) * grad])
    shp = [jax.ShapeDtypeStruct(x.shape, BF16), jax.ShapeDtypeStruct((2, x.shape[-1]), F32)]
    return stage_call(cid, True, False, local, part, (x, bias, scale, grad_y), shp)


def back_mid(cid, layer, part, x_mid, gain, grad_res, attn_sum, scale):
    def local(b, acc, ins, outs):
        x_ref, g_ref, r_ref, a_ref, s_ref = ins
        grad_in, x_hat = ln_bwd(acc, x_ref[b], row(g_ref, layer))
        grad_mid = r_ref[b].astype(F32) + grad_in
        outs[0][b] = grad_mid
        grad_attn = row(s_ref, layer) * grad_mid
        add_rows(outs[1], b, [acc * x_hat, acc, grad_mid * a_ref[b], grad_attn])
        return grad_attn.astype(BF16)
    shp = [jax.ShapeDtypeStruct(x_mid.shape, F32), jax.ShapeDtypeStruct((4, x_mid.shape[-1]), F32)]
    return stage_call(cid, True, True, local, part, (x_mid, gain, grad_res, attn_sum, scale), shp)


def back_in(cid, layer, part, x_in, gain, grad_mid, mlp_sum, scale):
    more = layer > 0

    def local(b, acc, ins, outs):
        x_ref, g_ref, m_ref = ins[:3]
        grad_in, x_hat = ln_bwd(acc, x_ref[b], row(g_ref, layer))
        grad = (m_ref[b] + grad_in).astype(BF16)
        outs[0][b] = grad
        sums = [acc * x_hat, acc]
        if not more:
            add_rows(outs[1], b, sums)
            return None
        grad = grad.astype(F32)
        grad_mlp = row(ins[4], layer - 1) * grad
        add_rows(outs[1], b, sums + [grad * ins[3][b], grad_mlp])
        return grad_mlp.astype(BF16)
    ins = (x_in, gain, grad_mid) + ((mlp_sum, scale) if more else ())
    shp = [jax.ShapeDtypeStruct(x_in.shape, BF16), jax.ShapeDtypeStruct((4 if more else 2, x_in.shape[-1]), F32)]
    return stage_call(cid, True, more, local, part, ins, shp)


def qkv_of(normed, w, b):
    return (dot('rd,kfd->krf', flat(normed), w) + b[:, None]).astype(BF16)


def mlp_up(normed, w_up, b_up):
    pre = dot('rd,cdf->crf', flat(normed), w_up) + b_up[:, None]
    return pre, (jax.nn.silu(pre[0]) * pre[1]).astype(BF16)


def mlp_bwd(grad_mlp, pre, w_down):
    grad_hidden = dot('rd,fd->rf', flat(grad_mlp), w_down)
    gate_sig = jax.nn.sigmoid(pre[0])
    grad_gate = grad_hidden * pre[1] * gate_sig * (1.0 + pre[0] * (1.0 - gate_sig))
    grad_lin = grad_hidden * pre[0] * gate_sig
    grad_pre = jnp.stack([grad_gate, grad_lin])
    return grad_pre.astype(BF16), jnp.sum(grad_pre, axis=1)


def device_fn(tokens, grad_y, valid_len, norm1_gain, norm1_bias, w_qkv, b_qkv, w_proj, b_proj, layer_scale1,
              norm2_gain, norm2_bias, w_up, b_up, w_down, b_down, layer_scale2):
    pad = ((0, 0), (0, PAD - TOK), (0, 0))
    x0 = jnp.pad(tokens, pad)
    g_y = jnp.pad(grad_y, pad)
    lens = (valid_len, swap_dp(valid_len))
    wq = w_qkv.transpose(0, 1, 3, 4, 2).reshape(2, 3, 256, 1024)
    bq = b_qkv.reshape(2, 3, 256)
    wp = w_proj.reshape(2, 256, 1024)

    x_in, x_mid, sum1, sum2, n1, n2, qkv, heads, pre, hid = ([None, None] for _ in range(10))
    x_in[0] = x0
    n1_own = gather_norm(0, 0, x0, norm1_gain, norm1_bias)
    gm_own = gather_scaled(1, 1, g_y, layer_scale2)
    gm = (gm_own, swap_dp(gm_own))
    for l in range(2):
        n1[l] = (n1_own, swap_dp(n1_own))
        qkv_own = qkv_of(n1[l][0], wq[l], bq[l])
        o_own = attn_fwd(qkv_own, lens[0])
        part = dot('rf,fd->rd', o_own, wp[l]).astype(BF16)
        x_mid[l], sum1[l], n2_own = residual_norm(2 + 3 * l, l, shards(part), x_in[l], b_proj, layer_scale1,
                                                  l, norm2_gain, norm2_bias)
        n2[l] = (n2_own, swap_dp(n2_own))
        qkv_oth = qkv_of(n1[l][1], wq[l], bq[l])
        o_oth = attn_fwd(qkv_oth, lens[1])
        qkv[l], heads[l] = (qkv_own, qkv_oth), (o_own, o_oth)
        pre_own, hid_own = mlp_up(n2[l][0], w_up[l], b_up[l])
        part = dot('rf,fd->rd', hid_own, w_down[l]).astype(BF16)
        if l == 0:
            x_in[1], sum2[0], n1_own = residual_norm(3, 0, shards(part), x_mid[0], b_down, layer_scale2,
                                                     1, norm1_gain, norm1_bias)
        else:
            y_out, rows_y = residual_last(4, 1, shards(part), x_mid[1], b_down, layer_scale2, g_y)
        pre_oth, hid_oth = mlp_up(n2[l][1], w_up[l], b_up[l])
        pre[l], hid[l] = (pre_own, pre_oth), (hid_own, hid_oth)

    grad_x = g_y
    rows_mlp = rows_y
    g_up = g_down = g_qkv = g_proj = None
    rows_by_layer, g_b_up, g_b_qkv = [None, None], [None, None], [None, None]
    for l in (1, 0):
        gp_own, gb_own = mlp_bwd(gm[0], pre[l][0], w_down[l])
        part = dot('crf,cdf->rd', gp_own, w_up[l]).astype(BF16)
        grad_mid, rows_mid, ga_own = back_mid(6 + 2 * (1 - l), l, shards(part), x_mid[l], norm2_gain, grad_x, sum1[l],
                                              layer_scale1)
        ga = (ga_own, swap_dp(ga_own))
        gp_oth, gb_oth = mlp_bwd(gm[1], pre[l][1], w_down[l])
        g_b_up[l] = gb_own + gb_oth
        g_down = wgrad(l, hid[l], [flat(g) for g in gm], lambda g, i: (0, i), lambda g, i: (0, 0), 1, 4, g_down, 'wg_down')
        g_up = wgrad(l, [flat(n) for n in n2[l]], (gp_own, gp_oth), lambda g, i: (0, i), lambda g, i: (g, 0, 0), 2, 4,
                     g_up, 'wg_up')
        do_own = dot('rd,fd->rf', flat(ga[0]), wp[l]).astype(BF16)
        gq_own, gbq_own = attn_bwd(qkv[l][0], do_own, lens[0])
        part = dot('krf,kfd->rd', gq_own, wq[l]).astype(BF16)
        res = back_in(7 + 2 * (1 - l), l, shards(part), x_in[l], norm1_gain, grad_mid, sum2[0], layer_scale2)
        do_oth = dot('rd,fd->rf', flat(ga[1]), wp[l]).astype(BF16)
        gq_oth, gbq_oth = attn_bwd(qkv[l][1], do_oth, lens[1])
        g_b_qkv[l] = gbq_own + gbq_oth
        g_proj = wgrad(l, heads[l], [flat(g) for g in ga], lambda g, i: (0, i), lambda g, i: (0, 0), 1, 1, g_proj, 'wg_proj')
        g_qkv = wgrad(l, (gq_own, gq_oth), [flat(n) for n in n1[l]], lambda g, i: (g, 0, 0), lambda g, i: (0, 0), 3, 1,
                      g_qkv, 'wg_qkv')
        grad_x = res[0]
        rows_by_layer[l] = [res[1][:2], rows_mid, rows_mlp]
        if l:
            rows_mlp = res[1][2:]
            gm = (res[2], swap_dp(res[2]))

    sums = lax.psum(jnp.concatenate(rows_by_layer[0] + rows_by_layer[1], axis=0), ('dp', 'tp')).reshape(2, 8, -1)
    n1g, n1b, n2g, n2b, ls1, bp, ls2, bd = (sums[:, k] for k in range(8))
    return (y_out[:, :TOK], grad_x[:, :TOK], n1g, n1b,
            g_qkv.reshape(2, 3, 4, 64, 1024).transpose(0, 1, 4, 2, 3), jnp.stack(g_b_qkv).reshape(2, 3, 4, 64),
            g_proj.reshape(2, 4, 64, 1024), bp, ls1, n2g, n2b, g_up, jnp.stack(g_b_up),
            g_down.reshape(2, 1024, 1024), bd, ls2)


def solution(mesh):
    rep = P()
    act = P('dp', 'tp', None)
    param_specs = (rep, rep, P(None, None, None, 'tp', None), P(None, None, 'tp', None), P(None, 'tp', None, None), rep,
                   rep, rep, rep, P(None, None, None, 'tp'), P(None, None, 'tp'), P(None, 'tp', None), rep, rep)
    return jax.shard_map(device_fn, mesh=mesh, in_specs=(act, act, P('dp')) + param_specs,
                         out_specs=(act, act) + param_specs, check_vma=False)
```

time: 1330 us -> 490 us (0.37)
  waiting for transfers between devices: 1030 us -> 97.8 us
  Pallas kernels: 0 us -> 255 us
  matrix products: 133 us -> 59.8 us
  other arithmetic: 72.4 us -> 11.8 us
  local copies, waits for them, and re-layouts: 62.6 us -> 32.3 us
    psum x2 -> x1, waiting for transfers between devices: 759 us -> 35.4 us  [device_fn(): lax.psum(jnp.concatenate(rows_by_layer[0] + rows_by_layer[1], axis=0), ('...]
    pallas_call x0 -> x26, Pallas kernels: none -> 255 us  [the longest x10 158 us: stage_call(): pl.pallas_call(kernel, out_shape=outs, in_specs=[vm] * len(args), out_spe...]
    unnamed x24 -> x1, waiting for transfers between devices: 190 us -> 0.02 us
    all_gather x8 -> x0, waiting for transfers between devices: 79.5 us -> none  [the longest x2 29 us: block_fwd(): normed_full = lax.all_gather(normed, 'tp', axis=1, tiled=True)]
    dot_general x36 -> x24, matrix products: 133 us -> 59.8 us  [dot(): return jnp.einsum(spec, a, b, preferred_element_type=F32)]
    ppermute x0 -> x9, waiting for transfers between devices: none -> 62.4 us  [swap_dp(): return lax.ppermute(x, 'dp', [(0, 1), (1, 0)])]
    reduce_sum x20 -> x2, other arithmetic: 32.7 us -> 2.82 us  [mlp_bwd(): return (grad_pre.astype(BF16), jnp.sum(grad_pre, axis=1))]
    unnamed x143 -> x208, local copies, waits for them, and re-layouts: 42.7 us -> 18.5 us
  transfers between devices with their start and end apart: 17 -> 10, of which waited for: 15 -> 4; matrix products, arithmetic and copies ran while one was open for 8% -> 16% of each run, Pallas kernels for 0% -> 31%
where the time goes in v2:
time: 490 us; the launch traced here: 482 us
  Pallas kernels  255 us (52%)
  waiting for transfers between devices  97.8 us (20%)
  matrix products  59.8 us (12%)
  local copies, waits for them, and re-layouts  32.3 us (7%)
  between operations  15.8 us (3%)
  other arithmetic  11.8 us (2%)
  starting transfers between devices  9.76 us (2%)
    pallas_call x10, Pallas kernels, stage_call(): pl.pallas_call(kernel, out_shape=outs, in_specs=[vm] * len(args), out_spe...  158 us
    ppermute x9, waiting for transfers between devices, swap_dp(): return lax.ppermute(x, 'dp', [(0, 1), (1, 0)])  62.4 us
    dot_general x24, matrix products, dot(): return jnp.einsum(spec, a, b, preferred_element_type=F32)  59.8 us
    pallas_call x8, Pallas kernels, wgrad(): pl.pallas_call(wgrad_kernel, grid=(groups, n_blk), in_specs=in_specs, out...  52 us
    psum x1, waiting for transfers between devices, device_fn(): lax.psum(jnp.concatenate(rows_by_layer[0] + rows_by_layer[1], axis=0), ('...  35.4 us
    pallas_call x4, Pallas kernels, attn_bwd(): pl.pallas_call(attn_bwd_kernel, grid=(n_seq,), in_specs=[pl.BlockSpec(mem...  27.4 us
    unnamed x208, local copies, waits for them, and re-layouts  18.5 us
    pallas_call x4, Pallas kernels, attn_fwd(): pl.pallas_call(attn_fwd_kernel, grid=(n_seq,), in_specs=[pl.BlockSpec(mem...  17.7 us
  transfers between devices with their start and end apart: 10, of which 4 were waited for; matrix products, arithmetic and copies ran while one was open for 16% of the time, Pallas kernels for 31%

profile of v2, /device:TPU:0, one launch (start us, length us, event | category | flops | bytes accessed | tf_op | source)
XLA Modules:
  0.0 481.8 jit_solution(11192036469595723756)
XLA Ops:
  14.3 12.5 %stage0.1 = bf16[2,4,72,1024]{3,2,1,0:T(8,128)(2,1)S(1)} custom-call(bf16[2,72,1024]{2,1,0:T(8,128)(2,1)S(1)} %pad.7.refs_0_.refs_1_, f32[2,1024]{1,0:T(2,128)S(1)} %copy-done.42, f32[2,1024]{1,0:T(2,128)S(1)} %copy-done.44), custom_call_target="tpu_custom_call" | custom-call | flops 40000000 | bytes 4000000 | tf_op jit(solution)/shard_map/stage0/pallas_call | solution.py:104
  28.1 4.3 attn_fwd.4.a0_ref
  33.6 19.2 %stage2.1 = (bf16[2,72,1024]{2,1,0:T(8,128)(2,1)S(1)}, f32[2,72,1024]{2,1,0:T(8,128)S(1)}, bf16[2,4,72,1024]{3,2,1,0:T(8,128)(2,1)}) custom-call(bf16[2,4,72,1024]{3,2,1,0:T(8,128)(2,1)S(1)} %bitcast.317, bf16[2,72,1024]{2,1,0:T(8,128)(2,1)S(1)} %pad.7.refs_0_.refs_1_, f32[2,1024]{1,0:T(2,128)S(1)} %copy-done.45, f32[2,1024]{1,0:T(2,128)S(1)} %copy-done.39, ...), custom_call_target="tpu_custom_call" | custom-call | flops 40000000 | bytes 4000000 | tf_op jit(solution)/shard_map/stage2/pallas_call | solution.py:104
  55.3 4.9 %add_bitcast_fusion.3 = f32[2,576,1024]{2,1,0:T(8,128)S(1)} fusion(f32[2,1024]{1,0:T(2,128)S(1)} %get-tuple-element.118, bf16[576,1024,1]{1,0,2:T(8,128)(2,1)} %bitcast.8, bf16[2,2,1024,1024]{3,2,1,0:T(8,128)(2,1)} %param.29), kind=kOutput, calls=%fused_computation.7 | convolution fusion | flops 2417098752 | bytes 10100736 | tf_op jit(solution)/shard_map/rd,cdf->crf/dot_general | solution.py:260
  61.7 19.3 %stage3.1 = (bf16[2,72,1024]{2,1,0:T(8,128)(2,1)S(1)}, f32[2,72,1024]{2,1,0:T(8,128)S(1)}, bf16[2,4,72,1024]{3,2,1,0:T(8,128)(2,1)}) custom-call(bf16[2,4,72,1024]{3,2,1,0:T(8,128)(2,1)S(1)} %bitcast.326, bf16[2,72,1024]{2,1,0:T(8,128)(2,1)S(1)} %get-tuple-element.47.refs_1_, f32[2,1024]{1,0:T(2,128)S(1)} %copy-done.47, f32[2,1024]{1,0:T(2,128)S(1)} %copy-done.41, ...), custom_call_target="tpu_custom_call" | custom-call | flops 40000000 | bytes 4000000 | tf_op jit(solution)/shard_map/stage3/pallas_call | solution.py:104
  83.6 4.5 attn_fwd.5.a0_ref
  88.8 19.2 %stage5.1 = (bf16[2,72,1024]{2,1,0:T(8,128)(2,1)S(1)}, f32[2,72,1024]{2,1,0:T(8,128)S(1)}, bf16[2,4,72,1024]{3,2,1,0:T(8,128)(2,1)}) custom-call(bf16[2,4,72,1024]{3,2,1,0:T(8,128)(2,1)S(1)} %bitcast.318, bf16[2,72,1024]{2,1,0:T(8,128)(2,1)S(1)} %get-tuple-element.49.refs_1_, f32[2,1024]{1,0:T(2,128)S(1)} %copy-done.45, f32[2,1024]{1,0:T(2,128)S(1)} %copy-done.39, ...), custom_call_target="tpu_custom_call" | custom-call | flops 40000000 | bytes 4000000 | tf_op jit(solution)/shard_map/stage5/pallas_call | solution.py:104
  108.6 10.3 %stage1.1 = bf16[2,4,72,1024]{3,2,1,0:T(8,128)(2,1)S(1)} custom-call(bf16[2,72,1024]{2,1,0:T(8,128)(2,1)S(1)} %pad.8.refs_4_.refs_0_.refs_3_, f32[2,1024]{1,0:T(2,128)S(1)} %copy-done.41), custom_call_target="tpu_custom_call" | custom-call | flops 40000000 | bytes 4000000 | tf_op jit(solution)/shard_map/stage1/pallas_call | solution.py:104
  118.9 4.3 add_bitcast_fusion.2
  132.9 19.2 %stage6.1 = (f32[2,72,1024]{2,1,0:T(8,128)S(1)}, f32[4,1024]{1,0:T(4,128)S(1)}, bf16[2,4,72,1024]{3,2,1,0:T(8,128)(2,1)}) custom-call(bf16[2,4,72,1024]{3,2,1,0:T(8,128)(2,1)S(1)} %bitcast.325, bf16[2,72,1024]{2,1,0:T(8,128)(2,1)S(1)} %get-tuple-element.51.refs_1_, f32[2,1024]{1,0:T(2,128)S(1)} %copy-done.40, ...), custom_call_target="tpu_custom_call" | custom-call | flops 40000000 | bytes 4000000 | tf_op jit(solution)/shard_map/stage6/pallas_call | solution.py:104
  153.9 7.0 %attn_bwd.4 = (bf16[3,576,256]{2,1,0:T(8,128)(2,1)S(1)}, f32[3,256]{1,0:T(4,128)S(1)}) custom-call(s32[2]{0:T(128)S(1)} %copy-done.58, bf16[3,576,256]{2,1,0:T(8,128)(2,1)S(1)} %fusion.85.qkv_ref, bf16[576,256]{1,0:T(8,128)(2,1)S(1)} %convolution_convert_fusion.5.do_ref), custom_call_target="tpu_custom_call" | custom-call | flops 4000000000 | bytes 3000000 | tf_op jit(solution)/shard_map/attn_bwd/pallas_call | solution.py:214
  162.1 18.2 %stage7.1 = (bf16[2,72,1024]{2,1,0:T(8,128)(2,1)S(1)}, f32[4,1024]{1,0:T(4,128)S(1)}, bf16[2,4,72,1024]{3,2,1,0:T(8,128)(2,1)S(1)}) custom-call(bf16[2,4,72,1024]{3,2,1,0:T(8,128)(2,1)S(1)} %bitcast.328, bf16[2,72,1024]{2,1,0:T(8,128)(2,1)S(1)} %get-tuple-element.49.refs_1_, f32[2,1024]{1,0:T(2,128)S(1)} %copy-done.43, ...), custom_call_target="tpu_custom_call" | custom-call | flops 40000000 | bytes 4000000 | tf_op jit(solution)/shard_map/stage7/pallas_call | solution.py:104
  188.6 18.2 %stage8.1 = (f32[2,72,1024]{2,1,0:T(8,128)S(1)}, f32[4,1024]{1,0:T(4,128)S(1)}, bf16[2,4,72,1024]{3,2,1,0:T(8,128)(2,1)S(1)}) custom-call(bf16[2,4,72,1024]{3,2,1,0:T(8,128)(2,1)S(1)} %bitcast.324, bf16[2,72,1024]{2,1,0:T(8,128)(2,1)S(1)} %copy-done.20, f32[2,1024]{1,0:T(2,128)S(1)} %copy-done.40, bf16[2,72,1024]{2,1,0:T(8,128)(2,1)S(1)} %get-tuple-element.59.refs_3_, ...), custom_call_target="tpu_custom_call" | custom-call | flops 40000000 | bytes 4000000 | tf_op jit(solution)/shard_map/stage8/pallas_call | solution.py:104
  208.3 11.0 %stage4.1 = (bf16[2,72,1024]{2,1,0:T(8,128)(2,1)S(1)}, f32[2,1024]{1,0:T(2,128)S(1)}) custom-call(bf16[2,4,72,1024]{3,2,1,0:T(8,128)(2,1)S(1)} %bitcast.323, bf16[2,72,1024]{2,1,0:T(8,128)(2,1)S(1)} %get-tuple-element.51.refs_1_, f32[2,1024]{1,0:T(2,128)S(1)} %copy-done.47, f32[2,1024]{1,0:T(2,128)S(1)} %copy-done.41, ...), custom_call_target="tpu_custom_call" | custom-call | flops 40000000 | bytes 4000000 | tf_op jit(solution)/shard_map/stage4/pallas_call | solution.py:104
  219.3 6.8 %attn_bwd.5 = (bf16[3,576,256]{2,1,0:T(8,128)(2,1)S(1)}, f32[3,256]{1,0:T(4,128)S(1)}) custom-call(s32[2]{0:T(128)S(1)} %copy-done.58, bf16[3,576,256]{2,1,0:T(8,128)(2,1)S(1)} %copy-done.60, bf16[576,256]{1,0:T(8,128)(2,1)S(1)} %convolution_convert_fusion.4.do_ref), custom_call_target="tpu_custom_call" | custom-call | flops 4000000000 | bytes 3000000 | tf_op jit(solution)/shard_map/attn_bwd/pallas_call | solution.py:214
  227.4 10.6 %stage9.1 = (bf16[2,72,1024]{2,1,0:T(8,128)(2,1)S(1)}, f32[2,1024]{1,0:T(2,128)S(1)}) custom-call(bf16[2,4,72,1024]{3,2,1,0:T(8,128)(2,1)S(1)} %bitcast.327, bf16[2,72,1024]{2,1,0:T(8,128)(2,1)S(1)} %copy-done.7, f32[2,1024]{1,0:T(2,128)S(1)} %copy-done.43, f32[2,72,1024]{2,1,0:T(8,128)S(1)} %get-tuple-element.63.refs_3_), custom_call_target="tpu_custom_call" | custom-call | flops 40000000 | bytes 4000000 | tf_op jit(solution)/shard_map/stage9/pallas_call | solution.py:104
  251.1 35.4 %all-reduce.4.cloned.1.call-done = f32[2,8,1024]{2,0,1:T(2,128)} async-done(((f32[2,8,1024]{2,0,1:T(2,128)}), f32[2,8,1024]{2,0,1:T(2,128)}) %all-reduce.4.cloned.1.call-update) | async-done | bytes 65552 | tf_op jit(solution)/shard_map/psum | solution.py:437
  288.8 4.8 add_bitcast_fusion.1
  294.8 4.9 %add_bitcast_fusion = f32[2,576,1024]{2,1,0:T(8,128)S(1)} fusion(f32[2,1024]{1,0:T(2,128)S(1)} %copy-done.92, bf16[576,1024,1]{1,0,2:T(8,128)(2,1)} %bitcast.77, bf16[2,2,1024,1024]{3,2,1,0:T(8,128)(2,1)} %param.29), kind=kOutput, calls=%fused_computation.4 | convolution fusion | flops 2417098752 | bytes 10100736 | tf_op jit(solution)/shard_map/rd,cdf->crf/dot_general | solution.py:260
  299.7 25.8 %collective-permute-done.6 = bf16[2,4,72,1024]{3,2,1,0:T(8,128)(2,1)S(1)} collective-permute-done((bf16[2,4,72,1024]{3,2,1,0:T(8,128)(2,1)}, bf16[2,4,72,1024]{3,2,1,0:T(8,128)(2,1)S(1)}, u32[]{:S(2)}, u32[]{:S(2)}) %collective-permute-start.6) | collective-permute-done | bytes 1179680 | tf_op jit(solution)/shard_map/ppermute | solution.py:264
  334.1 5.7 %multiply_bitcast_fusion.1 = (f32[1,576,1024]{2,1,0:T(8,128)}, f32[1,576,1024]{2,1,0:T(8,128)}, bf16[576,1024]{1,0:T(8,128)(2,1)}) fusion(f32[2,576,1024]{2,1,0:T(8,128)S(1)} %add_bitcast_fusion, bf16[576,1024]{1,0:T(8,128)(2,1)} %bitcast.76.b1_ref, bf16[2,1024,1024]{2,1,0:T(8,128)(2,1)S(1)} %copy-done.99), kind=kOutput, calls=%fused_computation.77 | convolution fusion | flops 1216217088 | bytes 13893632 | tf_op jit(solution)/shard_map/rd,fd->rf/dot_general | solution.py:260
  339.9 36.2 %collective-permute-done.2 = bf16[2,4,72,1024]{3,2,1,0:T(8,128)(2,1)S(1)} collective-permute-done((bf16[2,4,72,1024]{3,2,1,0:T(8,128)(2,1)S(1)}, bf16[2,4,72,1024]{3,2,1,0:T(8,128)(2,1)S(1)}, u32[]{:S(2)}, u32[]{:S(2)}) %collective-permute-start.2) | collective-permute-done | bytes 1179680 | tf_op jit(solution)/shard_map/ppermute | solution.py:264
  376.6 6.9 %attn_bwd.6 = (bf16[3,576,256]{2,1,0:T(8,128)(2,1)S(1)}, f32[3,256]{1,0:T(4,128)S(1)}) custom-call(s32[2]{0:T(128)S(1)} %collective-permute-done.vl_ref, bf16[3,576,256]{2,1,0:T(8,128)(2,1)S(1)} %fusion.86.qkv_ref, bf16[576,256]{1,0:T(8,128)(2,1)S(1)} %convolution_convert_fusion.3.do_ref), custom_call_target="tpu_custom_call" | custom-call | flops 4000000000 | bytes 3000000 | tf_op jit(solution)/shard_map/attn_bwd/pallas_call | solution.py:214
  385.1 4.4 fusion.15.b1_ref
  409.9 6.6 %attn_bwd.7 = (bf16[3,576,256]{2,1,0:T(8,128)(2,1)S(1)}, f32[3,256]{1,0:T(4,128)S(1)}) custom-call(s32[2]{0:T(128)S(1)} %collective-permute-done.vl_ref, bf16[3,576,256]{2,1,0:T(8,128)(2,1)S(1)} %fusion.87.qkv_ref, bf16[576,256]{1,0:T(8,128)(2,1)S(1)} %convolution_convert_fusion.2.do_ref), custom_call_target="tpu_custom_call" | custom-call | flops 4000000000 | bytes 3000000 | tf_op jit(solution)/shard_map/attn_bwd/pallas_call | solution.py:214
  420.1 4.5 attn_fwd.6.a1_ref
  428.0 6.6 %wg_down.2.rest_0_ = f32[2,1,1024,1024]{3,2,1,0:T(8,128)} custom-call(bf16[576,1024]{1,0:T(8,128)(2,1)S(1)} %copy-done.10, bf16[576,1024]{1,0:T(8,128)(2,1)S(1)} %copy-done.11, bf16[576,1024]{1,0:T(8,128)(2,1)S(1)} %bitcast.316, bf16[576,1024]{1,0:T(8,128)(2,1)} %bitcast.76.b1_ref), custom_call_target="tpu_custom_call" | custom-call | flops 2415919104 | bytes 8000000 | tf_op jit(solution)/shard_map/wg_down/pallas_call | solution.py:246
  434.6 5.8 %wg_qkv.2.rest_0_ = f32[2,3,256,1024]{3,2,1,0:T(8,128)} custom-call(bf16[3,576,256]{2,1,0:T(8,128)(2,1)S(1)} %copy-done.28, bf16[3,576,256]{2,1,0:T(8,128)(2,1)S(1)} %copy-done.30, bf16[576,1024]{1,0:T(8,128)(2,1)} %bitcast.15.b0_ref, bf16[576,1024]{1,0:T(8,128)(2,1)} %bitcast.56.b1_ref), custom_call_target="tpu_custom_call" | custom-call | flops 1811939328 | bytes 8000000 | tf_op jit(solution)/shard_map/wg_qkv/pallas_call | solution.py:246
  440.5 5.4 %wg_down.3 = f32[2,1,1024,1024]{3,2,1,0:T(8,128)} custom-call(bf16[576,1024]{1,0:T(8,128)(2,1)S(1)} %copy-done.23, bf16[576,1024]{1,0:T(8,128)(2,1)S(1)} %copy-done.26, bf16[576,1024]{1,0:T(8,128)(2,1)S(1)} %bitcast.330, bf16[576,1024]{1,0:T(8,128)(2,1)S(1)} %bitcast.332, f32[2,1,1024,1024]{3,2,1,0:T(8,128)} %wg_down.2.rest_0_), custom_call_target="tpu_custom_call", output_to_operand_aliasing={{}: (4, {})} | custom-call | flops 2415919104 | bytes 8000000 | tf_op jit(solution)/shard_map/wg_down/pallas_call | solution.py:246
  445.8 11.7 %wg_up.2.rest_0_ = f32[2,2,1024,1024]{3,2,1,0:T(8,128)} custom-call(bf16[576,1024]{1,0:T(8,128)(2,1)} %bitcast.21.a0_ref, bf16[576,1024]{1,0:T(8,128)(2,1)} %bitcast.75.a1_ref, bf16[2,576,1024]{2,1,0:T(8,128)(2,1)S(1)} %fusion.19.b0_ref, bf16[2,576,1024]{2,1,0:T(8,128)(2,1)S(1)} %copy-done.3), custom_call_target="tpu_custom_call" | custom-call | flops 4831838208 | bytes 8000000 | tf_op jit(solution)/shard_map/wg_up/pallas_call | solution.py:246
  457.5 5.4 %wg_qkv.3 = f32[2,3,256,1024]{3,2,1,0:T(8,128)} custom-call(bf16[3,576,256]{2,1,0:T(8,128)(2,1)S(1)} %copy-done.32, bf16[3,576,256]{2,1,0:T(8,128)(2,1)S(1)} %copy-done.34, bf16[576,1024]{1,0:T(8,128)(2,1)S(1)} %bitcast.314, bf16[576,1024]{1,0:T(8,128)(2,1)} %bitcast.52.b1_ref, f32[2,3,256,1024]{3,2,1,0:T(8,128)} %wg_qkv.2.rest_0_), custom_call_target="tpu_custom_call", output_to_operand_aliasing={{}: (4, {})} | custom-call | flops 1811939328 | bytes 8000000 | tf_op jit(solution)/shard_map/wg_qkv/pallas_call | solution.py:246
  463.0 11.5 %wg_up.3 = f32[2,2,1024,1024]{3,2,1,0:T(8,128)} custom-call(bf16[576,1024]{1,0:T(8,128)(2,1)} %bitcast.7.a0_ref, bf16[576,1024]{1,0:T(8,128)(2,1)} %bitcast.67.a1_ref, bf16[2,576,1024]{2,1,0:T(8,128)(2,1)S(1)} %copy-done.1, bf16[2,576,1024]{2,1,0:T(8,128)(2,1)S(1)} %copy-done.2, f32[2,2,1024,1024]{3,2,1,0:T(8,128)} %wg_up.2.rest_0_), custom_call_target="tpu_custom_call", output_to_operand_aliasing={{}: (4, {})} | custom-call | flops 4831838208 | bytes 8000000 | tf_op jit(solution)/shard_map/wg_up/pallas_call | solution.py:246
  (274 shorter events, 95.0 us)
Async XLA Ops:
  7.2 279.3 %all-reduce.4.cloned.1.call-start = ((), (), s32[]{:S(2)}) async-start(), calls=%async_computation | async-start | bytes 131072 | tf_op jit(solution)/shard_map/psum | solution.py:437
  8.0 18.8 %copy-start.96 = (f32[3,256]{1,0:T(4,128)}, f32[3,256]{1,0:T(4,128)S(1)}, u32[]{:S(2)}) copy-start(f32[3,256]{1,0:T(4,128)S(1)} %add.153) | copy-start | bytes 9220
  10.4 22.1 %copy-start.78 = (bf16[1,4,64,1024]{3,2,1,0:T(8,128)(2,1)}, bf16[1,4,64,1024]{3,2,1,0:T(8,128)(2,1)S(1)}, u32[]{:S(2)}) copy-start(bf16[1,4,64,1024]{3,2,1,0:T(8,128)(2,1)S(1)} %get-tuple-element.107) | copy-start | bytes 1572868
  10.4 77.8 %copy-start.75 = (bf16[1,4,64,1024]{3,2,1,0:T(8,128)(2,1)}, bf16[1,4,64,1024]{3,2,1,0:T(8,128)(2,1)S(1)}, u32[]{:S(2)}) copy-start(bf16[1,4,64,1024]{3,2,1,0:T(8,128)(2,1)S(1)} %get-tuple-element.106) | copy-start | bytes 1572868
  14.3 12.6 %copy-start.83 = (bf16[1,3,4,64,1024]{4,3,2,1,0:T(8,128)(2,1)}, bf16[1,3,4,64,1024]{4,3,2,1,0:T(8,128)(2,1)S(1)}, u32[]{:S(2)}) copy-start(bf16[1,3,4,64,1024]{4,3,2,1,0:T(8,128)(2,1)S(1)} %get-tuple-element.105) | copy-start | bytes 4718596
  14.3 19.3 %copy-start.6 = (bf16[2,72,1024]{2,1,0:T(8,128)(2,1)}, bf16[2,72,1024]{2,1,0:T(8,128)(2,1)S(1)}, u32[]{:S(2)}) copy-start(bf16[2,72,1024]{2,1,0:T(8,128)(2,1)S(1)} %pad.7.refs_0_.refs_1_) | copy-start | bytes 884740
  32.4 22.8 %copy-start.90 = (f32[2,2,1024]{2,1,0:T(2,128)S(1)}, f32[2,2,1024]{2,1,0:T(2,128)}, u32[]{:S(2)}) copy-start(f32[2,2,1024]{2,1,0:T(2,128)} %param.30) | copy-start | bytes 49156
  53.6 234.3 %collective-permute-start.5 = (bf16[2,4,72,1024]{3,2,1,0:T(8,128)(2,1)}, bf16[2,4,72,1024]{3,2,1,0:T(8,128)(2,1)}, u32[]{:S(2)}, u32[]{:S(2)}) collective-permute-start(bf16[2,4,72,1024]{3,2,1,0:T(8,128)(2,1)} %get-tuple-element.46), channel_id=1, source_target_pairs={{0,4},{4,0},{1,5},{5,1},{2,6},{6,2},{3,7},{7,3}} | collective-permute-start | bytes 3538952 | tf_op jit(solution)/shard_map/ppermute | solution.py:264
  55.2 25.7 %copy-start.94 = (f32[3,256]{1,0:T(4,128)}, f32[3,256]{1,0:T(4,128)S(1)}, u32[]{:S(2)}) copy-start(f32[3,256]{1,0:T(4,128)S(1)} %add.161) | copy-start | bytes 9220
  55.2 63.7 %copy-start.91 = (f32[2,1024]{1,0:T(2,128)}, f32[2,1024]{1,0:T(2,128)S(1)}, u32[]{:S(2)}) copy-start(f32[2,1024]{1,0:T(2,128)S(1)} %get-tuple-element.119) | copy-start | bytes 24580
  60.2 20.8 %copy-start.81 = (bf16[1,3,4,64,1024]{4,3,2,1,0:T(8,128)(2,1)S(1)}, bf16[1,3,4,64,1024]{4,3,2,1,0:T(8,128)(2,1)}, u32[]{:S(2)}) copy-start(bf16[1,3,4,64,1024]{4,3,2,1,0:T(8,128)(2,1)} %get-tuple-element.104) | copy-start | bytes 4718596
  81.0 37.9 %slice-start = ((s8[8388608]{0:T(1024)(128)(4,1)}), s8[4194304]{0:T(1024)(128)(4,1)S(1)}, s32[]{:S(2)}) async-start(s8[8388608]{0:T(1024)(128)(4,1)} %bitcast.352), calls=%async_computation.1 | async-start | bytes 8388608
  83.5 35.4 %slice-start.1 = ((s8[8388608]{0:T(1024)(128)(4,1)}), s8[4194304]{0:T(1024)(128)(4,1)S(1)}, s32[]{:S(2)}) async-start(s8[8388608]{0:T(1024)(128)(4,1)} %bitcast.352), calls=%async_computation.2 | async-start | bytes 8388608
  88.1 20.4 %copy-start.86 = (bf16[2,66,1024]{2,0,1:T(2,128)(2,1)S(1)}, bf16[2,66,1024]{2,0,1:T(2,128)(2,1)}, u32[]{:S(2)}) copy-start(bf16[2,66,1024]{2,0,1:T(2,128)(2,1)} %param.18) | copy-start | bytes 811012
  108.0 185.6 %collective-permute-start.7 = (bf16[2,4,72,1024]{3,2,1,0:T(8,128)(2,1)}, bf16[2,4,72,1024]{3,2,1,0:T(8,128)(2,1)}, u32[]{:S(2)}, u32[]{:S(2)}) collective-permute-start(bf16[2,4,72,1024]{3,2,1,0:T(8,128)(2,1)} %get-tuple-element.50), channel_id=1, source_target_pairs={{0,4},{4,0},{1,5},{5,1},{2,6},{6,2},{3,7},{7,3}} | collective-permute-start | bytes 3538952 | tf_op jit(solution)/shard_map/ppermute | solution.py:264
  132.9 19.2 %copy-start.76 = (bf16[1,4,64,1024]{3,2,1,0:T(8,128)(2,1)S(1)}, bf16[1,4,64,1024]{3,2,1,0:T(8,128)(2,1)}, u32[]{:S(2)}) copy-start(bf16[1,4,64,1024]{3,2,1,0:T(8,128)(2,1)} %copy-done.75) | copy-start | bytes 1572868
  132.9 21.0 %copy-start.58 = (s32[2]{0:T(128)S(1)}, s32[2]{0:T(128)}, u32[]{:S(2)}) copy-start(s32[2]{0:T(128)} %vl_ref.7) | copy-start | bytes 28
  188.6 19.2 %copy-start.79 = (bf16[1,4,64,1024]{3,2,1,0:T(8,128)(2,1)S(1)}, bf16[1,4,64,1024]{3,2,1,0:T(8,128)(2,1)}, u32[]{:S(2)}) copy-start(bf16[1,4,64,1024]{3,2,1,0:T(8,128)(2,1)} %copy-done.78) | copy-start | bytes 1572868
  206.8 19.4 %copy-start.50 = (f32[4,1024]{1,0:T(4,128)}, f32[4,1024]{1,0:T(4,128)S(1)}, u32[]{:S(2)}) copy-start(f32[4,1024]{1,0:T(4,128)S(1)} %get-tuple-element.66) | copy-start | bytes 49156
  206.8 12.5 %copy-start.60 = (bf16[3,576,256]{2,1,0:T(8,128)(2,1)S(1)}, bf16[3,576,256]{2,1,0:T(8,128)(2,1)}, u32[]{:S(2)}) copy-start(bf16[3,576,256]{2,1,0:T(8,128)(2,1)} %copy-done.59) | copy-start | bytes 2654212
  226.3 13.1 %copy-start.49 = (f32[4,1024]{1,0:T(4,128)S(1)}, f32[4,1024]{1,0:T(4,128)}, u32[]{:S(2)}) copy-start(f32[4,1024]{1,0:T(4,128)} %copy-done.48) | copy-start | bytes 49156
  243.7 132.9 %collective-permute-start = (s32[2]{0:T(128)}, s32[2]{0:T(128)S(1)}, u32[]{:S(2)}, u32[]{:S(2)}) collective-permute-start(s32[2]{0:T(128)} %vl_ref.7), channel_id=1, source_target_pairs={{0,4},{4,0},{1,5},{5,1},{2,6},{6,2},{3,7},{7,3}} | collective-permute-start | bytes 32 | tf_op jit(solution)/shard_map/ppermute | solution.py:264
  245.2 88.9 %collective-permute-start.8 = (bf16[2,4,72,1024]{3,2,1,0:T(8,128)(2,1)}, bf16[2,4,72,1024]{3,2,1,0:T(8,128)(2,1)}, u32[]{:S(2)}, u32[]{:S(2)}) collective-permute-start(bf16[2,4,72,1024]{3,2,1,0:T(8,128)(2,1)} %copy-done.4), channel_id=1, source_target_pairs={{0,4},{4,0},{1,5},{5,1},{2,6},{6,2},{3,7},{7,3}} | collective-permute-start | bytes 3538952 | tf_op jit(solution)/shard_map/ppermute | solution.py:264
  245.7 84.4 %collective-permute-start.1 = (bf16[2,4,72,1024]{3,2,1,0:T(8,128)(2,1)S(1)}, bf16[2,4,72,1024]{3,2,1,0:T(8,128)(2,1)}, u32[]{:S(2)}, u32[]{:S(2)}) collective-permute-start(bf16[2,4,72,1024]{3,2,1,0:T(8,128)(2,1)S(1)} %stage0.1), channel_id=1, source_target_pairs={{0,4},{4,0},{1,5},{5,1},{2,6},{6,2},{3,7},{7,3}} | collective-permute-start | bytes 3538952 | tf_op jit(solution)/shard_map/ppermute | solution.py:264
  288.0 37.5 %collective-permute-start.6 = (bf16[2,4,72,1024]{3,2,1,0:T(8,128)(2,1)}, bf16[2,4,72,1024]{3,2,1,0:T(8,128)(2,1)S(1)}, u32[]{:S(2)}, u32[]{:S(2)}) collective-permute-start(bf16[2,4,72,1024]{3,2,1,0:T(8,128)(2,1)} %copy-done.21), channel_id=1, source_target_pairs={{0,4},{4,0},{1,5},{5,1},{2,6},{6,2},{3,7},{7,3}} | collective-permute-start | bytes 3538952 | tf_op jit(solution)/shard_map/ppermute | solution.py:264
  293.6 103.7 %collective-permute-start.3 = (bf16[2,4,72,1024]{3,2,1,0:T(8,128)(2,1)}, bf16[2,4,72,1024]{3,2,1,0:T(8,128)(2,1)}, u32[]{:S(2)}, u32[]{:S(2)}) collective-permute-start(bf16[2,4,72,1024]{3,2,1,0:T(8,128)(2,1)} %get-tuple-element.48), channel_id=1, source_target_pairs={{0,4},{4,0},{1,5},{5,1},{2,6},{6,2},{3,7},{7,3}} | collective-permute-start | bytes 3538952 | tf_op jit(solution)/shard_map/ppermute | solution.py:264
  294.8 30.7 %copy-start.13 = (bf16[2,4,72,1024]{3,2,1,0:T(8,128)(2,1)S(1)}, bf16[2,4,72,1024]{3,2,1,0:T(8,128)(2,1)}, u32[]{:S(2)}) copy-start(bf16[2,4,72,1024]{3,2,1,0:T(8,128)(2,1)} %copy-done.12) | copy-start | bytes 3538948
  294.8 31.2 %copy-start.99 = (bf16[2,1024,1024]{2,1,0:T(8,128)(2,1)S(1)}, bf16[2,1024,1024]{2,1,0:T(8,128)(2,1)}, u32[]{:S(2)}) copy-start(bf16[2,1024,1024]{2,1,0:T(8,128)(2,1)} %param.31) | copy-start | bytes 12582916
  325.5 50.6 %collective-permute-start.2 = (bf16[2,4,72,1024]{3,2,1,0:T(8,128)(2,1)S(1)}, bf16[2,4,72,1024]{3,2,1,0:T(8,128)(2,1)S(1)}, u32[]{:S(2)}, u32[]{:S(2)}) collective-permute-start(bf16[2,4,72,1024]{3,2,1,0:T(8,128)(2,1)S(1)} %copy-done.13), channel_id=1, source_target_pairs={{0,4},{4,0},{1,5},{5,1},{2,6},{6,2},{3,7},{7,3}} | collective-permute-start | bytes 3538952 | tf_op jit(solution)/shard_map/ppermute | solution.py:264
  330.1 70.1 %collective-permute-start.4 = (bf16[2,4,72,1024]{3,2,1,0:T(8,128)(2,1)}, bf16[2,4,72,1024]{3,2,1,0:T(8,128)(2,1)}, u32[]{:S(2)}, u32[]{:S(2)}) collective-permute-start(bf16[2,4,72,1024]{3,2,1,0:T(8,128)(2,1)} %get-tuple-element.54), channel_id=1, source_target_pairs={{0,4},{4,0},{1,5},{5,1},{2,6},{6,2},{3,7},{7,3}} | collective-permute-start | bytes 3538952 | tf_op jit(solution)/shard_map/ppermute | solution.py:264
  334.1 42.5 %copy-start.61 = (bf16[3,576,256]{2,1,0:T(8,128)(2,1)}, bf16[3,576,256]{2,1,0:T(8,128)(2,1)S(1)}, u32[]{:S(2)}) copy-start(bf16[3,576,256]{2,1,0:T(8,128)(2,1)S(1)} %fusion.86.qkv_ref) | copy-start | bytes 2654212
  334.1 42.0 %copy-start.80 = (bf16[1,4,64,1024]{3,2,1,0:T(8,128)(2,1)S(1)}, bf16[1,4,64,1024]{3,2,1,0:T(8,128)(2,1)}, u32[]{:S(2)}) copy-start(bf16[1,4,64,1024]{3,2,1,0:T(8,128)(2,1)} %copy-done.78) | copy-start | bytes 1572868
  (80 other events, 315.1 us)
Sparse Core Ops, SparseCore 0:
  243.8 42.6 all-reduce.3
